TPU v7x, 8 devices: a whole 2x2x1 slice. The times are simulated.
8 devices in a mesh: layer: 1 (over z), tp: 2 (over y), fsdp: 4 (over x, core).
Axes of the slice: x: 2, y: 2, z: 1, core: 2. Of those that a mesh axis runs over, the one named last changes fastest.
Arguments:
- wq_weight: float32 [2048, 2048], P(('layer', 'fsdp'), 'tp')
- wq_moment: float32 [2048, 2048], P(('layer', 'fsdp'), 'tp')
- wq_grad: bfloat16 [2048, 2048], P(('layer', 'fsdp'), 'tp')
- wq_factor: float32 [2048, 128], P(('layer', 'tp'))
- wk_weight: float32 [2048, 2048], P(('layer', 'fsdp'), 'tp')
- wk_moment: float32 [2048, 2048], P(('layer', 'fsdp'), 'tp')
- wk_grad: bfloat16 [2048, 2048], P(('layer', 'fsdp'), 'tp')
- wk_factor: float32 [2048, 128], P(('layer', 'tp'))
- wv_weight: float32 [2048, 2048], P(('layer', 'fsdp'), 'tp')
- wv_moment: float32 [2048, 2048], P(('layer', 'fsdp'), 'tp')
- wv_grad: bfloat16 [2048, 2048], P(('layer', 'fsdp'), 'tp')
- wv_factor: float32 [2048, 128], P(('layer', 'tp'))
- wo_weight: float32 [2048, 2048], P(('layer', 'fsdp'), 'tp')
- wo_moment: float32 [2048, 2048], P(('layer', 'fsdp'), 'tp')
- wo_grad: bfloat16 [2048, 2048], P(('layer', 'fsdp'), 'tp')
- wo_factor: float32 [2048, 128], P(('layer', 'tp'))
- gate_weight: float32 [8, 2048, 1408], P('layer', 'fsdp', 'tp')
- gate_moment: float32 [8, 2048, 1408], P('layer', 'fsdp', 'tp')
- gate_grad: bfloat16 [8, 2048, 1408], P('layer', 'fsdp', 'tp')
- gate_factor: float32 [8, 1408, 88], P('layer', 'tp')
- up_weight: float32 [8, 2048, 1408], P('layer', 'fsdp', 'tp')
- up_moment: float32 [8, 2048, 1408], P('layer', 'fsdp', 'tp')
- up_grad: bfloat16 [8, 2048, 1408], P('layer', 'fsdp', 'tp')
- up_factor: float32 [8, 1408, 88], P('layer', 'tp')
- down_weight: float32 [8, 1408, 2048], P('layer', 'fsdp', 'tp')
- down_moment: float32 [8, 1408, 2048], P('layer', 'fsdp', 'tp')
- down_grad: bfloat16 [8, 1408, 2048], P('layer', 'fsdp', 'tp')
- down_factor: float32 [8, 1408, 88], P('layer', 'fsdp')
Outputs:
- output 1: float32 [2048, 2048], P(('layer', 'fsdp'), 'tp')
- output 2: float32 [2048, 2048], P(('layer', 'fsdp'), 'tp')
- output 3: float32 [2048, 128], P(('layer', 'tp'))
- output 4: float32 [2048, 2048], P(('layer', 'fsdp'), 'tp')
- output 5: float32 [2048, 2048], P(('layer', 'fsdp'), 'tp')
- output 6: float32 [2048, 128], P(('layer', 'tp'))
- output 7: float32 [2048, 2048], P(('layer', 'fsdp'), 'tp')
- output 8: float32 [2048, 2048], P(('layer', 'fsdp'), 'tp')
- output 9: float32 [2048, 128], P(('layer', 'tp'))
- output 10: float32 [2048, 2048], P(('layer', 'fsdp'), 'tp')
- output 11: float32 [2048, 2048], P(('layer', 'fsdp'), 'tp')
- output 12: float32 [2048, 128], P(('layer', 'tp'))
- output 13: float32 [8, 2048, 1408], P('layer', 'fsdp', 'tp')
- output 14: float32 [8, 2048, 1408], P('layer', 'fsdp', 'tp')
- output 15: float32 [8, 1408, 88], P('layer', 'tp')
- output 16: float32 [8, 2048, 1408], P('layer', 'fsdp', 'tp')
- output 17: float32 [8, 2048, 1408], P('layer', 'fsdp', 'tp')
- output 18: float32 [8, 1408, 88], P('layer', 'tp')
- output 19: float32 [8, 1408, 2048], P('layer', 'fsdp', 'tp')
- output 20: float32 [8, 1408, 2048], P('layer', 'fsdp', 'tp')
- output 21: float32 [8, 1408, 88], P('layer', 'fsdp')
All inputs are finite; a program needn't handle non-finite values.
Results may differ from a plain program's by a relative error of at most 0.001.
Values are sent between devices in bfloat16 or wider.
A program may use at most 1 GiB of HBM per device.

v0:
```python
import math
import jax
import jax.numpy as jnp
from jax import lax
from jax.sharding import PartitionSpec as P

MOMENTUM = 0.9
LEARN_RATE = 0.3
FULL_PREC = lax.Precision.HIGHEST
KEEP_FORMS = ('bmn,bnr->bmr', 'bmn,bmr->bnr', 'bmr,bnr->bmn')
FLIP_FORMS = ('bnm,bnr->bmr', 'bnm,bmr->bnr', 'bmr,bnr->bnm')


def mat_mul(form, left_op, right_op):
    return jnp.einsum(form, left_op, right_op, preferred_element_type=jnp.float32, precision=FULL_PREC)


def dion_local(weight, moment, gradient, factor, forms, long_axis, short_axis, long_size, short_size):
    mom_grad = moment + gradient.astype(jnp.float32)
    p_tilde = lax.psum(mat_mul(forms[0], mom_grad, factor), short_axis)
    gram_mat = lax.psum(mat_mul('bmr,bms->brs', p_tilde, p_tilde), long_axis)
    chol_low = jnp.linalg.cholesky(gram_mat)
    p_orth = lax.linalg.triangular_solve(chol_low, p_tilde, left_side=False, lower=True, transpose_a=True)
    r_new = lax.psum(mat_mul(forms[1], mom_grad, p_orth), long_axis)
    moment_new = mom_grad - (1.0 - MOMENTUM) * mat_mul(forms[2], p_orth, r_new)
    col_sq = lax.psum(jnp.sum(r_new * r_new, axis=1, keepdims=True), short_axis)
    factor_new = r_new / jnp.sqrt(col_sq)
    step_scale = LEARN_RATE * math.sqrt(p_tilde.shape[1] * long_size / (factor.shape[1] * short_size))
    weight_new = weight - step_scale * mat_mul(forms[2], p_orth, factor_new)
    return weight_new, moment_new, factor_new


def solution(mesh):
    fsdp_size = mesh.shape['fsdp']
    tp_size = mesh.shape['tp']
    dense_w = P(('layer', 'fsdp'), 'tp')
    dense_f = P(('layer', 'tp'), None)
    stack_w = P('layer', 'fsdp', 'tp')
    stack_f = P('layer', 'tp', None)
    down_f = P('layer', 'fsdp', None)
    in_specs = (dense_w, dense_w, dense_w, dense_f) * 4 + (stack_w, stack_w, stack_w, stack_f) * 2 + (stack_w, stack_w, stack_w, down_f)
    out_specs = (dense_w, dense_w, dense_f) * 4 + (stack_w, stack_w, stack_f) * 2 + (stack_w, stack_w, down_f)

    def local_step(*blocks):
        results = []
        for mat_idx in range(4):
            group_in = [local_arr[None] for local_arr in blocks[4 * mat_idx:4 * mat_idx + 4]]
            updated = dion_local(group_in[0], group_in[1], group_in[2], group_in[3], KEEP_FORMS, 'fsdp', 'tp', fsdp_size, tp_size)
            results.extend([item_out[0] for item_out in updated])
        for mat_idx in (4, 5):
            group_in = blocks[4 * mat_idx:4 * mat_idx + 4]
            results.extend(dion_local(group_in[0], group_in[1], group_in[2], group_in[3], KEEP_FORMS, 'fsdp', 'tp', fsdp_size, tp_size))
        group_in = blocks[24:28]
        results.extend(dion_local(group_in[0], group_in[1], group_in[2], group_in[3], FLIP_FORMS, 'tp', 'fsdp', tp_size, fsdp_size))
        return tuple(results)

    return jax.shard_map(local_step, mesh=mesh, in_specs=in_specs, out_specs=out_specs, check_vma=False)
```

profile of v0, /device:TPU:0, one launch (start us, length us, event | category | flops | bytes accessed | tf_op | source)
XLA Modules:
  0.0 1035.6 jit_solution(5644806923097311270)
XLA Ops:
  8.8 13.7 %fusion.1 = f32[8,512,88]{1,2,0:T(8,128)} fusion(f32[8,704,88]{1,2,0:T(8,128)S(1)} %copy-done, f32[8,512,704]{1,2,0:T(8,128)} %param.51, bf16[8,512,704]{1,2,0:T(8,128)(2,1)} %param.52), kind=kOutput, calls=%fused_computation.10 | convolution fusion | flops 3050831872 | bytes 20725760 | tf_op jit(solution)/shard_map/bmn,bnr->bmr/dot_general | solution.py:15
  36.5 16.0 %convolution_bitcast_fusion.8 = f32[1,512,128]{2,1,0:T(8,128)} fusion(f32[1024,128]{1,0:T(8,128)S(1)} %copy-done.63, f32[512,1024]{1,0:T(8,128)S(1)} %copy-done.13, bf16[512,1024]{1,0:T(8,128)(2,1)S(1)} %copy-done.23), kind=kOutput, calls=%fused_computation.37 | convolution fusion | flops 806354944 | bytes 3932160 | tf_op jit(solution)/shard_map/bmn,bnr->bmr/dot_general | solution.py:15
  55.0 13.9 %fusion.5 = f32[8,1024,88]{1,2,0:T(8,128)} fusion(f32[8,352,88]{1,2,0:T(8,128)} %param.61, f32[8,352,1024]{2,1,0:T(8,128)} %param.59, bf16[8,352,1024]{2,1,0:T(8,128)(2,1)} %param.60), kind=kOutput, calls=%fused_computation.14 | convolution fusion | flops 3050831872 | bytes 21176320 | tf_op jit(solution)/shard_map/bnm,bnr->bmr/dot_general | solution.py:15
  68.9 86.3 %all-reduce.18.cloned.1.call-done = (f32[1,512,128]{2,1,0:T(8,128)}, f32[1,512,128]{2,1,0:T(8,128)}, f32[1,512,128]{2,1,0:T(8,128)}, f32[1,512,128]{2,1,0:T(8,12...) async-done(((f32[1,512,128]{2,1,0:T(8,128)}, f32[1,512,128]{2,1,0:T(8,128)}, f32[1,512,128]{2,1,0:T(8,128)}, f32[1,512,128]{2,1,0:T(8,128)}, f32[8,512,88]{1,2,0:T(8,128)}, ...) | async-done | bytes 3932176 | tf_op jit(solution)/shard_map/psum | solution.py:20
  167.2 74.0 %all-reduce.16.cloned.1.call-done = (f32[1,128,128]{1,2,0:T(8,128)}, f32[1,128,128]{1,2,0:T(8,128)}, f32[1,128,128]{1,2,0:T(8,128)}, f32[1,128,128]{1,2,0:T(8,12...) async-done(((f32[1,128,128]{1,2,0:T(8,128)}, f32[1,128,128]{1,2,0:T(8,128)}, f32[1,128,128]{1,2,0:T(8,128)}, f32[1,128,128]{1,2,0:T(8,128)}, ...) | async-done | bytes 3641360 | tf_op jit(solution)/shard_map/psum | solution.py:21
  247.2 65.9 %custom-call.33 = f32[8,88,88]{2,1,0:T(8,128)} custom-call(f32[8,88,88]{2,1,0:T(8,128)} %get-tuple-element.57), custom_call_target="Cholesky" | custom-call | tf_op jit(solution)/shard_map/jit(cholesky)/cholesky | solution.py:22
  313.1 65.9 %custom-call.35 = f32[8,88,88]{2,1,0:T(8,128)} custom-call(f32[8,88,88]{2,1,0:T(8,128)} %get-tuple-element.56), custom_call_target="Cholesky" | custom-call | tf_op jit(solution)/shard_map/jit(cholesky)/cholesky | solution.py:22
  388.8 12.5 %custom-call.31 = f32[1,128,128]{2,1,0:T(8,128)S(1)} custom-call(f32[1,128,128]{2,1,0:T(8,128)} %get-tuple-element.58), custom_call_target="Cholesky" | custom-call | tf_op jit(solution)/shard_map/jit(cholesky)/cholesky | solution.py:22
  418.2 12.7 %custom-call.29 = f32[1,128,128]{2,1,0:T(8,128)S(1)} custom-call(f32[1,128,128]{2,1,0:T(8,128)} %get-tuple-element.59), custom_call_target="Cholesky" | custom-call | tf_op jit(solution)/shard_map/jit(cholesky)/cholesky | solution.py:22
  453.4 12.5 %custom-call.27 = f32[1,128,128]{2,1,0:T(8,128)S(1)} custom-call(f32[1,128,128]{2,1,0:T(8,128)} %get-tuple-element.60), custom_call_target="Cholesky" | custom-call | tf_op jit(solution)/shard_map/jit(cholesky)/cholesky | solution.py:22
  483.1 12.5 %custom-call.25 = f32[1,128,128]{2,1,0:T(8,128)S(1)} custom-call(f32[1,128,128]{2,1,0:T(8,128)} %get-tuple-element.61), custom_call_target="Cholesky" | custom-call | tf_op jit(solution)/shard_map/jit(cholesky)/cholesky | solution.py:22
  515.8 64.5 %custom-call.37 = f32[8,88,88]{2,1,0:T(8,128)S(1)} custom-call(f32[8,88,88]{2,1,0:T(8,128)S(1)} %fusion.12), custom_call_target="Cholesky" | custom-call | tf_op jit(solution)/shard_map/jit(cholesky)/cholesky | solution.py:22
  581.1 54.1 %custom-call.15 = f32[8,1,88,88]{2,3,1,0:T(8,128)S(1)} custom-call(f32[8,1,88,88]{3,2,1,0:T(8,128)S(1)} %get-tuple-element.53), custom_call_target="InvertDiagBlocksLowerTriangular" | custom-call | tf_op jit(solution)/shard_map/triangular_solve | solution.py:23
  641.3 15.4 %fusion.4 = f32[8,352,88]{1,2,0:T(8,128)} fusion(f32[8,1024,88]{1,2,0:T(8,128)S(1)} %fusion.10, f32[8,352,1024]{2,1,0:T(8,128)} %param.59, bf16[8,352,1024]{2,1,0:T(8,128)(2,1)} %param.60), kind=kOutput, calls=%fused_computation.13 | convolution fusion | flops 3050831872 | bytes 21176320 | tf_op jit(solution)/shard_map/bnm,bmr->bnr/dot_general | solution.py:15
  656.7 54.5 %custom-call.36 = f32[8,1,88,88]{2,3,1,0:T(8,128)S(1)} custom-call(f32[8,1,88,88]{3,2,1,0:T(8,128)S(1)} %get-tuple-element.54), custom_call_target="InvertDiagBlocksLowerTriangular" | custom-call | tf_op jit(solution)/shard_map/triangular_solve/custom-call.3 | solution.py:23
  714.0 16.6 %fusion.2 = f32[8,704,88]{1,2,0:T(8,128)} fusion(f32[8,512,88]{1,2,0:T(8,128)S(1)} %convolution_bitcast_fusion, f32[8,512,704]{1,2,0:T(8,128)} %param.55, bf16[8,512,704]{1,2,0:T(8,128)(2,1)} %param.56), kind=kOutput, calls=%fused_computation.11 | convolution fusion | flops 3050831872 | bytes 20725760 | tf_op jit(solution)/shard_map/bmn,bmr->bnr/dot_general | solution.py:15
  730.6 54.1 %custom-call.34 = f32[8,1,88,88]{2,3,1,0:T(8,128)S(1)} custom-call(f32[8,1,88,88]{3,2,1,0:T(8,128)S(1)} %get-tuple-element.55), custom_call_target="InvertDiagBlocksLowerTriangular" | custom-call | tf_op jit(solution)/shard_map/triangular_solve/custom-call.3 | solution.py:23
  788.5 16.8 %fusion = f32[8,704,88]{1,2,0:T(8,128)} fusion(f32[8,512,88]{1,2,0:T(8,128)S(1)} %convolution_bitcast_fusion.1, f32[8,512,704]{1,2,0:T(8,128)} %param.51, bf16[8,512,704]{1,2,0:T(8,128)(2,1)} %param.52), kind=kOutput, calls=%fused_computation.9 | convolution fusion | flops 3050831872 | bytes 20725760 | tf_op jit(solution)/shard_map/bmn,bmr->bnr/dot_general | solution.py:15
  815.6 16.2 %multiply_subtract_fusion.1 = f32[8,352,1024]{2,1,0:T(8,128)} fusion(f32[8,352,1024]{2,1,0:T(8,128)} %param.58, f32[8,352,88]{1,2,0:T(8,128)S(1)} %broadcast_divide_fusion.2, f32[8,1024,88]{1,2,0:T(8,128)} %copy-done.4), kind=kOutput, calls=%fused_computation.1 | convolution fusion | flops 3050831872 | bytes 26943488 | tf_op jit(solution)/shard_map/bmr,bnr->bnm/dot_general | solution.py:15
  831.8 16.6 %multiply_subtract_fusion = f32[8,352,1024]{2,1,0:T(8,128)} fusion(f32[8,352,1024]{2,1,0:T(8,128)} %param.59, bf16[8,352,1024]{2,1,0:T(8,128)(2,1)} %param.60, f32[8,352,88]{1,2,0:T(8,128)S(1)} %copy-done.19, f32[8,1024,88]{1,2,0:T(8,128)S(1)} %copy-done.5), kind=kOutput, calls=%fused_computation | convolution fusion | flops 3056599040 | bytes 32710656 | tf_op jit(solution)/shard_map/bmr,bnr->bnm/dot_general | solution.py:15
  848.4 73.4 %all-reduce.14.cloned.1.call-done = (f32[1,1024,128]{2,1,0:T(8,128)}, f32[1,1024,128]{2,1,0:T(8,128)}, f32[1,1024,128]{2,1,0:T(8,128)}, f32[1,1024,128]{2,1,0:T(...) async-done(((f32[1,1024,128]{2,1,0:T(8,128)}, f32[1,1024,128]{2,1,0:T(8,128)}, f32[1,1024,128]{2,1,0:T(8,128)}, f32[1,1024,128]{2,1,0:T(8,128)}, ...) | async-done | bytes 6062096 | tf_op jit(solution)/shard_map/psum | solution.py:24
  923.9 18.4 %multiply_subtract_fusion.2 = f32[8,512,704]{1,2,0:T(8,128)} fusion(f32[8,512,704]{1,2,0:T(8,128)} %param.55, bf16[8,512,704]{1,2,0:T(8,128)(2,1)} %param.56, f32[8,512,88]{1,2,0:T(8,128)S(1)} %convolution_bitcast_fusion, f32[8,704,88]{1,2,0:T(8,128)} %get-tuple-element.33), kind=kOutput, calls=%fused_computation.3 | convolution fusion | flops 3056599040 | bytes 32260096 | tf_op jit(solution)/shard_map/bmr,bnr->bmn/dot_general | solution.py:15
  944.3 15.1 %multiply_subtract_fusion.4 = f32[8,512,704]{1,2,0:T(8,128)} fusion(f32[8,512,704]{1,2,0:T(8,128)S(1)} %bitcast.228, bf16[8,512,704]{1,2,0:T(8,128)(2,1)S(1)} %bitcast.230, f32[8,512,88]{1,2,0:T(8,128)S(1)} %copy-done.7, f32[8,704,88]{1,2,0:T(8,128)} %get-tuple-element.32), kind=kOutput, calls=%fused_computation.6 | convolution fusion | flops 3056599040 | bytes 32260096 | tf_op jit(solution)/shard_map/bmr,bnr->bmn/dot_general | solution.py:15
  988.0 15.3 %multiply_subtract_fusion.3 = f32[8,512,704]{1,2,0:T(8,128)} fusion(f32[8,512,704]{1,2,0:T(8,128)} %param.54, f32[8,512,88]{1,2,0:T(8,128)S(1)} %convolution_bitcast_fusion, f32[8,704,88]{1,2,0:T(8,128)S(1)} %broadcast_divide_fusion), kind=kOutput, calls=%fused_computation.4 | convolution fusion | flops 3050831872 | bytes 26492928 | tf_op jit(solution)/shard_map/bmr,bnr->bmn/dot_general | solution.py:15
  (259 shorter events, 203.4 us)
Async XLA Ops:
  7.2 148.0 %all-reduce.18.cloned.1.call-start = ((), (), s32[]{:S(2)}) async-start(), calls=%async_computation.4 | async-start | bytes 7864320 | tf_op jit(solution)/shard_map/psum | solution.py:20
  36.4 16.0 %copy-start.16 = (f32[512,1024]{1,0:T(8,128)S(1)}, f32[512,1024]{1,0:T(8,128)}, u32[]{:S(2)}) copy-start(f32[512,1024]{1,0:T(8,128)} %param.35) | copy-start | bytes 6291460
  36.5 16.0 %copy-start.26 = (bf16[512,1024]{1,0:T(8,128)(2,1)S(1)}, bf16[512,1024]{1,0:T(8,128)(2,1)}, u32[]{:S(2)}) copy-start(bf16[512,1024]{1,0:T(8,128)(2,1)} %param.36) | copy-start | bytes 3145732
  55.0 186.2 %all-reduce.16.cloned.1.call-start = ((), (), s32[]{:S(2)}) async-start(), calls=%async_computation.3 | async-start | bytes 7733248 | tf_op jit(solution)/shard_map/psum | solution.py:21
  166.6 347.1 %all-reduce.10.cloned.1.call-start = ((), (), s32[]{:S(2)}) async-start(), calls=%async_computation | async-start | bytes 720896 | tf_op jit(solution)/shard_map/psum | solution.py:21
  385.4 419.9 %all-reduce.12.cloned.1.call-start = ((), (), s32[]{:S(2)}) async-start(), calls=%async_computation.1 | async-start | bytes 2162688 | tf_op jit(solution)/shard_map/psum | solution.py:24
  444.1 34.7 %copy-start.14 = (f32[512,1024]{1,0:T(8,128)S(1)}, f32[512,1024]{1,0:T(8,128)}, u32[]{:S(2)}) copy-start(f32[512,1024]{1,0:T(8,128)} %param.39) | copy-start | bytes 6291460
  444.1 34.7 %copy-start.24 = (bf16[512,1024]{1,0:T(8,128)(2,1)S(1)}, bf16[512,1024]{1,0:T(8,128)(2,1)}, u32[]{:S(2)}) copy-start(bf16[512,1024]{1,0:T(8,128)(2,1)} %param.40) | copy-start | bytes 3145732
  507.2 73.1 %copy-start.55 = (f32[8,88,88]{2,1,0:T(8,128)S(1)}, f32[8,88,88]{2,1,0:T(8,128)}, u32[]{:S(2)}) copy-start(f32[8,88,88]{2,1,0:T(8,128)} %custom-call.33) | copy-start | bytes 743428
  507.2 73.1 %copy-start.56 = (f32[8,88,88]{2,1,0:T(8,128)S(1)}, f32[8,88,88]{2,1,0:T(8,128)}, u32[]{:S(2)}) copy-start(f32[8,88,88]{2,1,0:T(8,128)} %custom-call.35) | copy-start | bytes 743428
  507.3 73.1 %copy-start.69 = (pred[88,88]{1,0:T(8,128)(4,1)S(1)}, pred[88,88]{1,0:T(8,128)(4,1)}, u32[]{:S(2)}) copy-start(pred[88,88]{1,0:T(8,128)(4,1)} %iota_compare_fusion.3) | copy-start | bytes 23236
  656.7 265.1 %all-reduce.14.cloned.1.call-start = ((), (), s32[]{:S(2)}) async-start(), calls=%async_computation.2 | async-start | bytes 12845056 | tf_op jit(solution)/shard_map/psum | solution.py:24
  815.6 16.2 %copy-start.5 = (f32[8,1024,88]{1,2,0:T(8,128)S(1)}, f32[8,1024,88]{1,2,0:T(8,128)}, u32[]{:S(2)}) copy-start(f32[8,1024,88]{1,2,0:T(8,128)} %copy-done.4) | copy-start | bytes 8650756
  815.6 16.2 %copy-start.19 = (f32[8,352,88]{1,2,0:T(8,128)S(1)}, f32[8,352,88]{1,2,0:T(8,128)}, u32[]{:S(2)}) copy-start(f32[8,352,88]{1,2,0:T(8,128)} %all-reduce.12.cloned.1.call-done) | copy-start | bytes 2973700
  921.8 22.4 %slice-start = ((s8[11534336]{0:T(1024)(128)(4,1)}), s8[4194304]{0:T(1024)(128)(4,1)S(1)}, s32[]{:S(2)}) async-start(s8[11534336]{0:T(1024)(128)(4,1)} %bitcast.227), calls=%async_computation.5 | async-start | bytes 8388608
  921.8 22.4 %slice-start.3 = ((s8[5767168]{0:T(1024)(128)(4,1)}), s8[4194304]{0:T(1024)(128)(4,1)S(1)}, s32[]{:S(2)}) async-start(s8[5767168]{0:T(1024)(128)(4,1)} %bitcast.229), calls=%async_computation.8 | async-start | bytes 8388608
  923.8 20.4 %slice-start.1 = ((s8[11534336]{0:T(1024)(128)(4,1)}), s8[4194304]{0:T(1024)(128)(4,1)S(1)}, s32[]{:S(2)}) async-start(s8[11534336]{0:T(1024)(128)(4,1)} %bitcast.227), calls=%async_computation.6 | async-start | bytes 8388608
  923.8 20.4 %slice-start.2 = ((s8[11534336]{0:T(1024)(128)(4,1)}), s8[3145728]{0:T(1024)(128)(4,1)S(1)}, s32[]{:S(2)}) async-start(s8[11534336]{0:T(1024)(128)(4,1)} %bitcast.227), calls=%async_computation.7 | async-start | bytes 6291456
  923.9 20.4 %slice-start.4 = ((s8[5767168]{0:T(1024)(128)(4,1)}), s8[1572864]{0:T(1024)(128)(4,1)S(1)}, s32[]{:S(2)}) async-start(s8[5767168]{0:T(1024)(128)(4,1)} %bitcast.229), calls=%async_computation.9 | async-start | bytes 3145728
  986.4 16.9 %copy-start.29 = (f32[8,704,88]{1,2,0:T(8,128)}, f32[8,704,88]{1,2,0:T(8,128)S(1)}, u32[]{:S(2)}) copy-start(f32[8,704,88]{1,2,0:T(8,128)S(1)} %broadcast_divide_fusion.1) | copy-start | bytes 5947396
  987.7 28.2 %copy-start.47 = (f32[1024,128]{1,0:T(8,128)}, f32[1024,128]{1,0:T(8,128)S(1)}, u32[]{:S(2)}) copy-start(f32[1024,128]{1,0:T(8,128)S(1)} %divide_bitcast_fusion) | copy-start | bytes 1572868
  987.7 31.4 %copy-start.48 = (f32[1024,128]{1,0:T(8,128)}, f32[1024,128]{1,0:T(8,128)S(1)}, u32[]{:S(2)}) copy-start(f32[1024,128]{1,0:T(8,128)S(1)} %divide_bitcast_fusion.1) | copy-start | bytes 1572868
  987.8 34.5 %copy-start.49 = (f32[1024,128]{1,0:T(8,128)}, f32[1024,128]{1,0:T(8,128)S(1)}, u32[]{:S(2)}) copy-start(f32[1024,128]{1,0:T(8,128)S(1)} %divide_bitcast_fusion.2) | copy-start | bytes 1572868
  987.9 37.7 %copy-start.50 = (f32[1024,128]{1,0:T(8,128)}, f32[1024,128]{1,0:T(8,128)S(1)}, u32[]{:S(2)}) copy-start(f32[1024,128]{1,0:T(8,128)S(1)} %divide_bitcast_fusion.3) | copy-start | bytes 1572868
  (59 other events, 351.6 us)
Sparse Core Ops, SparseCore 0:
  55.1 100.0 all-reduce.17
  166.7 74.5 all-reduce.15
  385.5 19.7 all-reduce.9
  656.8 35.4 all-reduce.11
  805.4 116.3 all-reduce.13
where the time goes:
time: 1040 us
  other arithmetic  472 us (45%)
  matrix products  284 us (27%)
  waiting for transfers between devices  234 us (22%)
  local copies, waits for them, and re-layouts  15.6 us (2%)
  between operations  15.1 us (1%)
  blocking collectives  14.5 us (1%)
    dot_general x35, matrix products, mat_mul(): jnp.einsum(form, left_op, right_op, preferred_element_type=jnp.float32, p...  270 us
    another operation x20, other arithmetic, dion_local(): chol_low = jnp.linalg.cholesky(gram_mat)  250 us
    another operation x13, other arithmetic, dion_local(): lax.linalg.triangular_solve(chol_low, p_tilde, left_side=False, lower=Tru...  205 us
    psum x1, waiting for transfers between devices, dion_local(): p_tilde = lax.psum(mat_mul(forms[0], mom_grad, factor), short_axis)  86.3 us
    psum x2, waiting for transfers between devices, dion_local(): gram_mat = lax.psum(mat_mul('bmr,bms->brs', p_tilde, p_tilde), long_axis)  74 us
    psum x2, waiting for transfers between devices, dion_local(): r_new = lax.psum(mat_mul(forms[1], mom_grad, p_orth), long_axis)  73.4 us
  transfers between devices with their start and end apart: 5, of which 3 were waited for; matrix products, arithmetic and copies ran while one was open for 31% of the time, Pallas kernels for 0%

commit v1 on v0

v1 whole, which is shorter than its diff:
```python
import math
import jax
import jax.numpy as jnp
from jax import lax
from jax.experimental import pallas as pl
from jax.experimental.pallas import tpu as pltpu
from jax.sharding import PartitionSpec as P

MOMENTUM = 0.9
LEARN_RATE = 0.3
FULL_PREC = lax.Precision.HIGHEST
LANES = 128
BF = jnp.bfloat16
F32 = jnp.float32


def split3(x):
    hi = x.astype(BF)
    rest = x - hi.astype(F32)
    mid = rest.astype(BF)
    low = (rest - mid.astype(F32)).astype(BF)
    return hi, mid, low


def eliminate(a_ref, li_ref, rank):
    lane = lax.broadcasted_iota(jnp.int32, (8, LANES), 1)
    for k0 in range(0, rank, 8):
        def step(kk, carry, k0=k0):
            k = k0 + kk
            row = a_ref[k]
            at_k = lane == k
            idx = jnp.full((8, LANES), k, jnp.int32)
            piv = jnp.take_along_axis(row, idx, axis=1)
            rinv = 1.0 / piv
            scaled = jnp.where(at_k, rinv, row * rinv)
            rs = 1.0 / jnp.sqrt(piv)
            li_ref[k] = jnp.where(at_k, rs, jnp.where(lane < k, row * rs, 0.0))
            for i in range(k0 + 1, rank):
                cur = a_ref[i]
                g = jnp.take_along_axis(cur, idx, axis=1)
                new = jnp.where(at_k, 0.0, cur) - g * scaled
                if i < k0 + 8:
                    new = jnp.where(i > k, new, cur)
                a_ref[i] = new
            return carry
        lax.fori_loop(0, 8, step, 0)


def chol_kernel(we_ref, wd_ref, le_ref, ld_ref, ae, ad):
    ae[...] = we_ref[...]
    ad[...] = wd_ref[...]
    for g in range(3):
        eliminate(ae.at[g], le_ref.at[g], 88)
    eliminate(ad, ld_ref, 128)


def chol_inverse(we, wd):
    return pl.pallas_call(
        chol_kernel,
        out_shape=(jax.ShapeDtypeStruct(we.shape, F32), jax.ShapeDtypeStruct(wd.shape, F32)),
        scratch_shapes=[pltpu.VMEM(we.shape, F32), pltpu.VMEM(wd.shape, F32)],
        name='chol_inverse',
    )(we, wd)


def pad_rows(x):
    rank, cols = x.shape
    if rank == LANES:
        return x
    return jnp.concatenate([x, jnp.zeros((LANES - rank, cols), F32)], axis=0)


def left_cat(ut):
    h, m, l = split3(pad_rows(ut).T)
    return jnp.concatenate([h, h, m, m, h, l], axis=1)


def right_cat(vt):
    h, m, l = split3(pad_rows(vt))
    return jnp.concatenate([l, h, m, h, m, h], axis=0)


def left_cat2(ut):
    h, m, l = split3(pad_rows(ut).T)
    return jnp.concatenate([h, l, m, m, h, h], axis=1)


def update_block(x_ref, m_ref, g_ref, ut, vt, dinv, x_out, m_out, scale):
    left = left_cat2(ut)
    b = m_ref[...] + g_ref[...].astype(F32)
    m_out[...] = b - (1.0 - MOMENTUM) * jnp.dot(left, right_cat(vt), preferred_element_type=F32)
    x_out[...] = x_ref[...] - scale * jnp.dot(left, right_cat(vt * dinv), preferred_element_type=F32)


def update_kernel(flips, scales, *refs):
    n = len(flips)
    ins, outs = refs[:6 * n], refs[6 * n:]
    for i in range(n):
        x_ref, m_ref, g_ref, pt_ref, rt_ref, d_ref = ins[6 * i:6 * i + 6]
        x_out, m_out, q_out = outs[3 * i:3 * i + 3]
        pt, rt, dinv = pt_ref[0], rt_ref[0], d_ref[0]
        ut, vt = (rt, pt) if flips[i] else (pt, rt)
        if len(x_ref.shape) == 3:
            x_ref, m_ref, g_ref, x_out, m_out, q_out = (r.at[0] for r in (x_ref, m_ref, g_ref, x_out, m_out, q_out))
        update_block(x_ref, m_ref, g_ref, ut, vt, dinv, x_out, m_out, scales[i])
        if len(x_ref.shape) == 2 and q_out.shape[0] == rt.shape[1]:
            q_out[...] = pad_rows(rt * dinv).T[:, :rt.shape[0]]


def expert_update(mats, scales):
    in_specs, out_specs, out_shape, args = [], [], [], []
    for x, m, g, pt, rt, d in mats:
        for arr in (x, m, g, pt, rt, d):
            in_specs.append(pl.BlockSpec((1,) + arr.shape[1:], lambda e: (e, 0, 0)))
            args.append(arr)
        q_shape = (rt.shape[0], rt.shape[2], rt.shape[1])
        for shape in (x.shape, x.shape, q_shape):
            out_specs.append(pl.BlockSpec((1,) + shape[1:], lambda e: (e, 0, 0)))
            out_shape.append(jax.ShapeDtypeStruct(shape, F32))

    def body(*refs):
        update_kernel((False, False, True), scales, *refs)

    return pl.pallas_call(
        body, grid=(8,), in_specs=in_specs, out_specs=out_specs, out_shape=out_shape,
        compiler_params=pltpu.CompilerParams(vmem_limit_bytes=60 * 2 ** 20),
        name='expert_update',
    )(*args)


def dense_body(scale, *refs):
    for i in range(4):
        x_ref, m_ref, g_ref, pt_ref, rt_ref, d_ref = refs[6 * i:6 * i + 6]
        x_out, m_out, q_out = refs[24 + 3 * i:27 + 3 * i]
        rt, dinv = rt_ref[0], d_ref[0]
        update_block(x_ref, m_ref, g_ref, pt_ref[0], rt, dinv, x_out, m_out, scale)
        part = pl.program_id(0)
        q_rows = q_out.shape[0]
        q_out[...] = (rt_ref[0, :, pl.ds(pl.multiple_of(part * q_rows, q_rows), q_rows)] * dinv).T


def dense_update(mats, scale):
    in_specs, out_specs, out_shape, args = [], [], [], []
    steps = 4
    for x, m, g, pt, rt, d in mats:
        rows, cols = x.shape
        blk = pl.BlockSpec((rows // steps, cols), lambda s: (s, 0))
        in_specs += [blk, blk, blk,
                     pl.BlockSpec((1, 128, rows // steps), lambda s: (0, 0, s)),
                     pl.BlockSpec(rt.shape, lambda s: (0, 0, 0)),
                     pl.BlockSpec(d.shape, lambda s: (0, 0, 0))]
        args += [x, m, g, pt, rt, d]
        out_specs += [blk, blk, pl.BlockSpec((cols // steps, 128), lambda s: (s, 0))]
        out_shape += [jax.ShapeDtypeStruct(x.shape, F32)] * 2 + [jax.ShapeDtypeStruct((cols, 128), F32)]

    def body(*refs):
        dense_body(scale, *refs)

    return pl.pallas_call(
        body, grid=(steps,), in_specs=in_specs, out_specs=out_specs, out_shape=out_shape,
        compiler_params=pltpu.CompilerParams(vmem_limit_bytes=60 * 2 ** 20),
        name='dense_update',
    )(*args)


def mat_mul(form, left_op, right_op):
    return jnp.einsum(form, left_op, right_op, preferred_element_type=F32, precision=FULL_PREC)


def solution(mesh):
    dense_w = P(('layer', 'fsdp'), 'tp')
    dense_f = P(('layer', 'tp'), None)
    stack_w = P('layer', 'fsdp', 'tp')
    stack_f = P('layer', 'tp', None)
    down_f = P('layer', 'fsdp', None)
    in_specs = (dense_w, dense_w, dense_w, dense_f) * 4 + (stack_w, stack_w, stack_w, stack_f) * 2 + (stack_w, stack_w, stack_w, down_f)
    out_specs = (dense_w, dense_w, dense_f) * 4 + (stack_w, stack_w, stack_f) * 2 + (stack_w, stack_w, down_f)

    def local_step(*blocks):
        mats = []
        for i in range(7):
            w, m, g, q = blocks[4 * i:4 * i + 4]
            if i < 4:
                w, m, g, q = w[None], m[None], g[None], q[None]
            b = m + g.astype(F32)
            flip = i == 6
            pt = mat_mul('bnr,bnm->brm' if flip else 'bnr,bmn->brm', q, b)
            pt = lax.psum(pt, 'fsdp' if flip else 'tp')
            gram = mat_mul('brm,bsm->brs', pt, pt)
            st = mat_mul('brm,bnm->brn' if flip else 'brm,bmn->brn', pt, b)
            gram, st = lax.psum((gram, st), 'tp' if flip else 'fsdp')
            mats.append([w, m, g, pt, st, gram])
        lane_pad = ((0, 0), (0, 0), (0, 0), (0, 40))
        we = jnp.stack([mats[i][5].transpose(1, 0, 2) for i in (4, 5, 6)])
        we = jnp.pad(we, lane_pad)
        wd = jnp.concatenate([mats[i][5] for i in (0, 1, 2, 3, 0, 1, 2, 3)]).transpose(1, 0, 2)
        le, ld = chol_inverse(we, wd)
        le = le.transpose(0, 2, 1, 3)[..., :88]
        ld = ld.transpose(1, 0, 2)
        ready = []
        sq = []
        for i in range(7):
            w, m, g, pt, st, _ = mats[i]
            linv = ld[i:i + 1] if i < 4 else le[i - 4]
            pt = mat_mul('brs,bsm->brm', linv, pt)
            rt = mat_mul('brs,bsn->brn', linv, st)
            ready.append([w, m, g, pt, rt])
            sq.append(jnp.sum(rt * rt, axis=2, keepdims=True))
        keep_sq = lax.psum(tuple(sq[:6]), 'tp')
        down_sq = lax.psum(sq[6], 'fsdp')
        for i in range(7):
            total = keep_sq[i] if i < 6 else down_sq
            ready[i].append(1.0 / jnp.sqrt(total))
        scale_e = LEARN_RATE * math.sqrt(2048 / 1408)
        results = []
        dense = [[r[0][0], r[1][0], r[2][0], r[3], r[4], r[5]] for r in ready[:4]]
        results.extend(dense_update(dense, LEARN_RATE))
        results.extend(expert_update(ready[4:], (scale_e,) * 3))
        return tuple(results)

    return jax.shard_map(local_step, mesh=mesh, in_specs=in_specs, out_specs=out_specs, check_vma=False)
```

time: 1040 us -> 744 us (0.72)
  other arithmetic: 472 us -> 2.15 us
  matrix products: 284 us -> 151 us
  Pallas kernels: 0 us -> 129 us
  local copies, waits for them, and re-layouts: 15.6 us -> 134 us
  waiting for transfers between devices: 234 us -> 264 us
  blocking collectives: 14.5 us -> 41.4 us
    another operation x37 -> x1, other arithmetic: 456 us -> 2.15 us  [local_step(): we = jnp.stack([mats[i][5].transpose(1, 0, 2) for i in (4, 5, 6)])]
    pallas_call x0 -> x3, Pallas kernels: none -> 129 us  [the longest x1 58.4 us: expert_update(): pl.pallas_call(body, grid=(8,), in_specs=in_specs, out_specs=out_specs, o...]
    dot_general x35, matrix products: 270 us -> 151 us  [mat_mul(): jnp.einsum(form, left_op, right_op, preferred_element_type=F32, precision...]
    unnamed x156 -> x111, local copies, waits for them, and re-layouts: 7.71 us -> 123 us
    psum x5 -> x3, waiting for transfers between devices: 234 us -> 264 us  [the longest x2 264 us: local_step(): pt = lax.psum(pt, 'fsdp' if flip else 'tp')]
    psum x2, blocking collectives: 14.5 us -> 41.4 us  [the longest x1 25.9 us: local_step(): keep_sq = lax.psum(tuple(sq[:6]), 'tp')]
    another operation x7 -> x0, matrix products: 14.5 us -> none  [dion_local(): lax.linalg.triangular_solve(chol_low, p_tilde, left_side=False, lower=Tru...]
  transfers between devices with their start and end apart: 5 -> 3, of which waited for: 3 -> 2; matrix products, arithmetic and copies ran while one was open for 31% -> 11% of each run, Pallas kernels for 0% -> 0%
where the time goes in v1:
time: 744 us; the launch traced here: 736 us
  waiting for transfers between devices  264 us (35%)
  matrix products  151 us (20%)
  local copies, waits for them, and re-layouts  134 us (18%)
  Pallas kernels  129 us (17%)
  blocking collectives  41.4 us (6%)
  between operations  14.5 us (2%)
    psum x2, waiting for transfers between devices, local_step(): pt = lax.psum(pt, 'fsdp' if flip else 'tp')  264 us
    dot_general x35, matrix products, mat_mul(): jnp.einsum(form, left_op, right_op, preferred_element_type=F32, precision...  151 us
    unnamed x111, local copies, waits for them, and re-layouts  123 us
    pallas_call x1, Pallas kernels, expert_update(): pl.pallas_call(body, grid=(8,), in_specs=in_specs, out_specs=out_specs, o...  58.4 us
    pallas_call x1, Pallas kernels, chol_inverse(): pl.pallas_call(chol_kernel, out_shape=(jax.ShapeDtypeStruct(we.shape, F32...  54.2 us
    psum x1, blocking collectives, local_step(): keep_sq = lax.psum(tuple(sq[:6]), 'tp')  25.9 us
    pallas_call x1, Pallas kernels, dense_update(): pl.pallas_call(body, grid=(steps,), in_specs=in_specs, out_specs=out_spec...  16.7 us
    psum x1, blocking collectives, local_step(): down_sq = lax.psum(sq[6], 'fsdp')  15.4 us
  transfers between devices with their start and end apart: 3, of which 2 were waited for; matrix products, arithmetic and copies ran while one was open for 11% of the time, Pallas kernels for 0%

profile of v1, /device:TPU:0, one launch (start us, length us, event | category | flops | bytes accessed | tf_op | source)
XLA Modules:
  0.0 736.2 jit_solution(14962280736276925266)
XLA Ops:
  24.5 10.8 %fusion.8 = f32[8,88,512]{2,1,0:T(8,128)} fusion(f32[8,704,88]{1,2,0:T(8,128)S(1)} %copy-done, f32[8,512,704]{1,2,0:T(8,128)S(1)} %copy-done.2, bf16[8,512,704]{1,2,0:T(8,128)(2,1)} %param.46), kind=kOutput, calls=%fused_computation.17 | convolution fusion | flops 3050831872 | bytes 20725760 | tf_op jit(solution)/shard_map/bnr,bmn->brm/dot_general | solution.py:167
  35.3 11.9 %fusion.7 = f32[8,88,512]{2,1,0:T(8,128)} fusion(f32[8,704,88]{1,2,0:T(8,128)} %param.51, f32[8,512,704]{1,2,0:T(8,128)S(1)} %bitcast.116, bf16[8,512,704]{1,2,0:T(8,128)(2,1)} %param.50), kind=kOutput, calls=%fused_computation.16 | convolution fusion | flops 3050831872 | bytes 20725760 | tf_op jit(solution)/shard_map/bnr,bmn->brm/dot_general | solution.py:167
  47.3 14.4 %fusion.6 = f32[8,88,1024]{2,1,0:T(8,128)} fusion(f32[8,352,88]{1,2,0:T(8,128)} %param.55, f32[8,352,1024]{2,1,0:T(8,128)} %refs_13_.3, bf16[8,352,1024]{2,1,0:T(8,128)(2,1)} %refs_14_.3), kind=kOutput, calls=%fused_computation.15 | convolution fusion | flops 3050831872 | bytes 21176320 | tf_op jit(solution)/shard_map/bnr,bnm->brm/dot_general | solution.py:167
  61.7 85.6 %all-reduce.13.cloned.1.call-done = (f32[8,88,512]{2,1,0:T(8,128)}, f32[8,88,512]{2,1,0:T(8,128)}, f32[128,512]{0,1:T(8,128)}, f32[128,512]{0,1:T(8,128)}, f32[128,512]{0,1:T(8,128)}, /*index=5*/f32[128,512]{0,1:T(8,128)}) async-done(((f32[8,88,512]{2,1,0:T(8,128)}, f32[8,88,512]{2,1,0:T(8,128)}, f32[128,512]{0,1:T(8,128)}, f32[128,512]{0,1:T(8,128)}, f32[128,512]{0,1:T(8,128)}, ...) | async-done | bytes 3932176 | tf_op jit(solution)/shard_map/psum | solution.py:188
  164.8 16.9 %fusion.2 = f32[8,88,704]{2,1,0:T(8,128)} fusion(f32[8,88,512]{2,1,0:T(8,128)S(1)} %copy-done.6, f32[8,512,704]{1,2,0:T(8,128)} %param.49, bf16[8,512,704]{1,2,0:T(8,128)(2,1)} %param.50), kind=kOutput, calls=%fused_computation.5 | convolution fusion | flops 3050831872 | bytes 20725760 | tf_op jit(solution)/shard_map/brm,bmn->brn/dot_general | solution.py:167
  183.2 11.8 %fusion = f32[8,88,704]{2,1,0:T(8,128)} fusion(f32[8,88,512]{2,1,0:T(8,128)S(1)} %copy-done.5, f32[8,512,704]{1,2,0:T(8,128)S(1)} %bitcast.114, bf16[8,512,704]{1,2,0:T(8,128)(2,1)S(1)} %bitcast.118), kind=kOutput, calls=%fused_computation.3 | convolution fusion | flops 3050831872 | bytes 20725760 | tf_op jit(solution)/shard_map/brm,bmn->brn/dot_general | solution.py:167
  196.1 178.1 %all-reduce.9.cloned.1.call-done = (f32[8,88,1024]{2,1,0:T(8,128)}, f32[1,88,8,88]{3,2,1,0:T(8,128)}, f32[1,88,8,88]{3,2,1,0:T(8,128)}, f32[1,128,128]{2,0,1:T(1...) async-done(((f32[8,88,1024]{2,1,0:T(8,128)}, ...) | async-done | bytes 9703440 | tf_op jit(solution)/shard_map/psum | solution.py:188
  374.2 5.6 fusion.36
  379.8 15.3 %fusion.4 = f32[8,88,352]{2,1,0:T(8,128)} fusion(f32[8,88,1024]{2,1,0:T(8,128)S(1)} %copy-done.3, f32[8,352,1024]{2,1,0:T(8,128)} %refs_13_.3, bf16[8,352,1024]{2,1,0:T(8,128)(2,1)} %refs_14_.3), kind=kOutput, calls=%fused_computation.7 | convolution fusion | flops 3050831872 | bytes 21176320 | tf_op jit(solution)/shard_map/brm,bnm->brn/dot_general | solution.py:167
  396.0 8.4 %copy.93.refs_2_ = bf16[8,512,704]{2,1,0:T(8,128)(2,1)} copy(bf16[8,512,704]{1,2,0:T(8,128)(2,1)} %param.46) | data formatting | bytes 11534336 | tf_op args[18]
  404.4 8.4 %copy.96.refs_8_ = bf16[8,512,704]{2,1,0:T(8,128)(2,1)} copy(bf16[8,512,704]{1,2,0:T(8,128)(2,1)} %param.50) | data formatting | bytes 11534336 | tf_op args[22]
  412.8 12.3 %copy.92.refs_1_ = f32[8,512,704]{2,1,0:T(8,128)} copy(f32[8,512,704]{1,2,0:T(8,128)} %param.45) | data formatting | bytes 23068672 | tf_op args[17]
  425.1 12.2 %copy.95.refs_7_ = f32[8,512,704]{2,1,0:T(8,128)} copy(f32[8,512,704]{1,2,0:T(8,128)} %param.49) | data formatting | bytes 23068672 | tf_op args[21]
  437.3 12.3 %copy.91.refs_0_ = f32[8,512,704]{2,1,0:T(8,128)} copy(f32[8,512,704]{1,2,0:T(8,128)} %param.44) | data formatting | bytes 23068672 | tf_op args[16]
  449.6 12.3 %copy.94.refs_6_ = f32[8,512,704]{2,1,0:T(8,128)} copy(f32[8,512,704]{1,2,0:T(8,128)} %param.48) | data formatting | bytes 23068672 | tf_op args[20]
  465.6 54.2 %chol_inverse.1 = (f32[3,88,8,128]{3,2,1,0:T(8,128)}, f32[128,8,128]{2,1,0:T(8,128)}) custom-call(f32[3,88,8,128]{3,2,1,0:T(8,128)} %select_maximum_fusion.we_ref, f32[128,8,128]{2,1,0:T(8,128)} %bitcast.123), custom_call_target="tpu_custom_call" | custom-call | tf_op jit(solution)/shard_map/chol_inverse/pallas_call | solution.py:58
  550.9 25.9 %all-reduce.2 = (f32[1,128,1]{2,1,0:T(8,128)S(1)}, f32[1,128,1]{2,1,0:T(8,128)S(1)}, f32[1,128,1]{2,1,0:T(8,128)S(1)}, f32[1,128,1]{2,1,0:T(8,128)S(1)}, f32[8,8...) all-reduce(f32[1,128,1]{2,1,0:T(8,128)S(1)} %copy.78, ...), channel_id=1, replica_groups=mesh['layer'=1,'tp'=2,'fsdp'=4] {'tp'}, use_global_device_ids=true, to_apply=%region_16.0 | all-reduce | flops 1920 | bytes 15360 | tf_op jit(solution)/shard_map/psum | solution.py:209
  579.6 15.4 %psum.223 = f32[8,88,1]{2,1,0:T(8,128)S(1)} all-reduce(f32[8,88,1]{2,1,0:T(8,128)S(1)} %copy.90), channel_id=1, replica_groups=mesh['layer'=1,'tp'=2,'fsdp'=4] {'fsdp'}, use_global_device_ids=true, to_apply=%region_34.35 | all-reduce | flops 704 | bytes 5632 | tf_op jit(solution)/shard_map/psum | solution.py:210
  597.4 58.4 %expert_update.1 = (f32[8,512,704]{2,1,0:T(8,128)}, f32[8,512,704]{2,1,0:T(8,128)}, f32[8,704,88]{2,1,0:T(8,128)}, f32[8,512,704]{2,1,0:T(8,128)}, f32[8,512,704...) custom-call(f32[8,512,704]{2,1,0:T(8,128)} %copy.91.refs_0_, ...), custom_call_target="tpu_custom_call" | custom-call | tf_op jit(solution)/shard_map/expert_update/pallas_call | solution.py:124
  655.9 12.3 %copy.97 = f32[8,512,704]{1,2,0:T(8,128)} copy(f32[8,512,704]{2,1,0:T(8,128)} %get-tuple-element.100) | data formatting | bytes 23068672
  676.1 12.2 %copy.98 = f32[8,512,704]{1,2,0:T(8,128)} copy(f32[8,512,704]{2,1,0:T(8,128)} %get-tuple-element.101) | data formatting | bytes 23068672
  688.3 12.2 %copy.100 = f32[8,512,704]{1,2,0:T(8,128)} copy(f32[8,512,704]{2,1,0:T(8,128)} %get-tuple-element.103) | data formatting | bytes 23068672
  700.5 12.2 %copy.101 = f32[8,512,704]{1,2,0:T(8,128)} copy(f32[8,512,704]{2,1,0:T(8,128)} %get-tuple-element.104) | data formatting | bytes 23068672
  712.7 16.7 %dense_update.1 = (f32[512,1024]{1,0:T(8,128)}, f32[512,1024]{1,0:T(8,128)}, f32[1024,128]{1,0:T(8,128)}, f32[512,1024]{1,0:T(8,128)}, f32[512,1024]{1,0:T(8,128...) custom-call(f32[512,1024]{1,0:T(8,128)} %refs_0_.2, ...), custom_call_target="tpu_custom_call" | custom-call | tf_op jit(solution)/shard_map/dense_update/pallas_call | solution.py:159
  (159 shorter events, 85.8 us)
Async XLA Ops:
  7.2 17.3 %copy-start = (f32[8,704,88]{1,2,0:T(8,128)S(1)}, f32[8,704,88]{1,2,0:T(8,128)}, u32[]{:S(2)}) copy-start(f32[8,704,88]{1,2,0:T(8,128)} %param.47) | copy-start | bytes 5947396
  7.2 140.1 %all-reduce.13.cloned.1.call-start = ((), (), s32[]{:S(2)}) async-start(), calls=%async_computation.2 | async-start | bytes 7864320 | tf_op jit(solution)/shard_map/psum | solution.py:188
  11.9 12.6 %copy-start.2 = (f32[8,512,704]{1,2,0:T(8,128)S(1)}, f32[8,512,704]{1,2,0:T(8,128)}, u32[]{:S(2)}) copy-start(f32[8,512,704]{1,2,0:T(8,128)} %param.45) | copy-start | bytes 34603012
  19.9 15.5 %slice-start.3 = ((s8[11534336]{0:T(1024)(128)(4,1)}), s8[4194304]{0:T(1024)(128)(4,1)S(1)}, s32[]{:S(2)}) async-start(s8[11534336]{0:T(1024)(128)(4,1)} %bitcast.115), calls=%async_computation.6 | async-start | bytes 8388608
  47.2 102.4 %copy-start.8 = (f32[512,1024]{1,0:T(8,128)S(1)}, f32[512,1024]{1,0:T(8,128)}, u32[]{:S(2)}) copy-start(f32[512,1024]{1,0:T(8,128)} %refs_1_.2) | copy-start | bytes 6291460
  47.2 102.3 %copy-start.13 = (bf16[512,1024]{1,0:T(8,128)(2,1)S(1)}, bf16[512,1024]{1,0:T(8,128)(2,1)}, u32[]{:S(2)}) copy-start(bf16[512,1024]{1,0:T(8,128)(2,1)} %refs_2_.2) | copy-start | bytes 3145732
  47.2 327.0 %all-reduce.9.cloned.1.call-start = ((), (), s32[]{:S(2)}) async-start(), calls=%async_computation | async-start | bytes 20578304 | tf_op jit(solution)/shard_map/psum | solution.py:188
  163.3 19.9 %slice-start = ((s8[11534336]{0:T(1024)(128)(4,1)}), s8[4194304]{0:T(1024)(128)(4,1)S(1)}, s32[]{:S(2)}) async-start(s8[11534336]{0:T(1024)(128)(4,1)} %bitcast.113), calls=%async_computation.3 | async-start | bytes 8388608
  163.3 19.9 %slice-start.6 = ((s8[5767168]{0:T(1024)(128)(4,1)}), s8[4194304]{0:T(1024)(128)(4,1)S(1)}, s32[]{:S(2)}) async-start(s8[5767168]{0:T(1024)(128)(4,1)} %bitcast.117), calls=%async_computation.9 | async-start | bytes 8388608
  164.7 17.0 %copy-start.5 = (f32[8,88,512]{2,1,0:T(8,128)S(1)}, f32[8,88,512]{2,1,0:T(8,128)}, u32[]{:S(2)}) copy-start(f32[8,88,512]{2,1,0:T(8,128)} %get-tuple-element.131) | copy-start | bytes 4325380
  164.7 18.4 %slice-start.1 = ((s8[11534336]{0:T(1024)(128)(4,1)}), s8[4194304]{0:T(1024)(128)(4,1)S(1)}, s32[]{:S(2)}) async-start(s8[11534336]{0:T(1024)(128)(4,1)} %bitcast.113), calls=%async_computation.4 | async-start | bytes 8388608
  164.7 18.4 %slice-start.2 = ((s8[11534336]{0:T(1024)(128)(4,1)}), s8[3145728]{0:T(1024)(128)(4,1)S(1)}, s32[]{:S(2)}) async-start(s8[11534336]{0:T(1024)(128)(4,1)} %bitcast.113), calls=%async_computation.5 | async-start | bytes 6291456
  164.8 18.4 %slice-start.7 = ((s8[5767168]{0:T(1024)(128)(4,1)}), s8[1572864]{0:T(1024)(128)(4,1)S(1)}, s32[]{:S(2)}) async-start(s8[5767168]{0:T(1024)(128)(4,1)} %bitcast.117), calls=%async_computation.10 | async-start | bytes 3145728
  196.0 267.4 %all-reduce.11.cloned.1.call-start = ((), (), s32[]{:S(2)}) async-start(), calls=%async_computation.1 | async-start | bytes 2883584 | tf_op jit(solution)/shard_map/psum | solution.py:191
  449.6 12.4 %copy-start.38 = (f32[1,128,128]{2,0,1:T(1,128)S(1)}, f32[1,128,128]{2,0,1:T(1,128)}, u32[]{:S(2)}) copy-start(f32[1,128,128]{2,0,1:T(1,128)} %get-tuple-element.113) | copy-start | bytes 196612
  449.6 12.4 %copy-start.39 = (f32[1,128,128]{2,0,1:T(1,128)S(1)}, f32[1,128,128]{2,0,1:T(1,128)}, u32[]{:S(2)}) copy-start(f32[1,128,128]{2,0,1:T(1,128)} %get-tuple-element.114) | copy-start | bytes 196612
  449.6 12.4 %copy-start.40 = (f32[1,128,128]{2,0,1:T(1,128)S(1)}, f32[1,128,128]{2,0,1:T(1,128)}, u32[]{:S(2)}) copy-start(f32[1,128,128]{2,0,1:T(1,128)} %get-tuple-element.115) | copy-start | bytes 196612
  449.6 13.9 %copy-start.35 = (f32[1,88,8,88]{3,2,1,0:T(8,128)S(1)}, f32[1,88,8,88]{3,2,1,0:T(8,128)}, u32[]{:S(2)}) copy-start(f32[1,88,8,88]{3,2,1,0:T(8,128)} %get-tuple-element.110) | copy-start | bytes 743428
  449.6 13.8 %copy-start.36 = (f32[1,88,8,88]{3,2,1,0:T(8,128)S(1)}, f32[1,88,8,88]{3,2,1,0:T(8,128)}, u32[]{:S(2)}) copy-start(f32[1,88,8,88]{3,2,1,0:T(8,128)} %get-tuple-element.111) | copy-start | bytes 743428
  463.5 58.4 %copy-start.25 = (f32[128,512]{0,1:T(8,128)S(1)}, f32[128,512]{0,1:T(8,128)}, u32[]{:S(2)}) copy-start(f32[128,512]{0,1:T(8,128)} %get-tuple-element.132) | copy-start | bytes 786436
  463.5 59.5 %copy-start.24 = (f32[128,512]{0,1:T(8,128)S(1)}, f32[128,512]{0,1:T(8,128)}, u32[]{:S(2)}) copy-start(f32[128,512]{0,1:T(8,128)} %get-tuple-element.133) | copy-start | bytes 786436
  465.6 58.4 %copy-start.22 = (f32[128,512]{0,1:T(8,128)S(1)}, f32[128,512]{0,1:T(8,128)}, u32[]{:S(2)}) copy-start(f32[128,512]{0,1:T(8,128)} %get-tuple-element.134) | copy-start | bytes 786436
  465.6 59.5 %copy-start.34 = (f32[128,1024]{1,0:T(8,128)S(1)}, f32[128,1024]{1,0:T(8,128)}, u32[]{:S(2)}) copy-start(f32[128,1024]{1,0:T(8,128)} %get-tuple-element.118) | copy-start | bytes 1572868
  712.7 16.7 %copy-start.1 = (f32[8,704,88]{1,2,0:T(8,128)S(1)}, f32[8,704,88]{1,2,0:T(8,128)}, u32[]{:S(2)}) copy-start(f32[8,704,88]{1,2,0:T(8,128)} %param.47) | copy-start | bytes 5947396
  (28 other events, 145.4 us)
Sparse Core Ops, SparseCore 0:
  47.3 99.9 all-reduce.12
  196.2 177.9 all-reduce.8
  396.1 43.2 all-reduce.10

commit v2 on v0

v2 whole, which is shorter than its diff:
```python
import math
import jax
import jax.numpy as jnp
from jax import lax
from jax.experimental import pallas as pl
from jax.experimental.pallas import tpu as pltpu
from jax.sharding import PartitionSpec as P

MOMENTUM = 0.9
LEARN_RATE = 0.3
LANES = 128
BF = jnp.bfloat16
F32 = jnp.float32
MIB = 2 ** 20
NN = (((1,), (0,)), ((), ()))
NT = (((1,), (1,)), ((), ()))
MESH = pl.DeviceIdType.MESH


def split3(x):
    hi = x.astype(BF)
    rest = x - hi.astype(F32)
    mid = rest.astype(BF)
    low = (rest - mid.astype(F32)).astype(BF)
    return hi, mid, low


def rows_to(x, rows):
    have, cols = x.shape
    if have == rows:
        return x
    return jnp.concatenate([x, jnp.zeros((rows - have, cols), x.dtype)], axis=0)


def dot6(left, right, dims):
    rank = left.shape[0]
    pad = -(-rank // 16) * 16
    lh, lm, ll = split3(rows_to(left, pad))
    rh, rm, rl = split3(right)
    with_h = lax.dot_general(jnp.concatenate([lh, lm, ll], axis=0), rh, dims, preferred_element_type=F32)
    with_m = lax.dot_general(jnp.concatenate([lh, lm], axis=0), rm, dims, preferred_element_type=F32)
    with_l = lax.dot_general(lh, rl, dims, preferred_element_type=F32)
    small = with_h[2 * pad:2 * pad + rank] + with_m[pad:pad + rank] + with_l[:rank]
    mid = with_h[pad:pad + rank] + with_m[:rank]
    return (small + mid) + with_h[:rank]


def exchange_kernel(*refs):
    em, eg, eq = refs[0:9:3], refs[1:9:3], refs[2:9:3]
    dm, dg, dq = refs[9:21:3], refs[10:21:3], refs[11:21:3]
    o_pk, o_pf, o_sf, o_sd, o_pd, o_sfd = refs[21:27]
    (mk, gk, qk, md, gd, qd, mw, gw, qw,
     pk, pk_in, pd, pd_c, pd_x, pf, sk, sk_c, sk_x, sf, sd, sd_in,
     pw, pw_in, sw, sw_c, sw_x, sfw,
     ld, ldw, ldq, out_sem, outw_sem, remote, remote_w) = refs[27:]
    t = lax.axis_index('tp')
    f = lax.axis_index('fsdp')
    c = lax.rem(f, 2)
    y_dev = {'tp': 1 - t}
    c_dev = {'fsdp': f + 1 - 2 * c}
    x_dev = {'fsdp': lax.rem(f + 2, 4)}
    bar = pltpu.get_barrier_semaphore()
    for dev in (y_dev, c_dev, x_dev):
        pl.semaphore_signal(bar, inc=1, device_id=dev, device_id_type=MESH)

    def expert_load(j, e, with_q):
        m_buf, g_buf, q_buf = (mk.at[j], gk.at[j], qk.at[j]) if j < 2 else (md, gd, qd)
        copies = [pltpu.make_async_copy(em[j].at[e], m_buf, ld.at[j, 0]),
                  pltpu.make_async_copy(eg[j].at[e], g_buf, ld.at[j, 1])]
        if with_q:
            copies.append(pltpu.make_async_copy(eq[j].at[e], q_buf, ld.at[j, 2]))
        return copies

    def start_all(copies):
        for cp in copies:
            cp.start()

    def wait_all(copies):
        for cp in copies:
            cp.wait()

    def dense_load(i, s):
        h, slot = lax.rem(s, 2), lax.rem(s, 2)
        rows = pl.ds(pl.multiple_of(h * 256, 256), 256)
        return [pltpu.make_async_copy(dm[i].at[rows], mw.at[slot], ldw.at[slot, 0]),
                pltpu.make_async_copy(dg[i].at[rows], gw.at[slot], ldw.at[slot, 1])]

    def dense_q(i, s):
        slot = lax.rem(s // 2, 2)
        return pltpu.make_async_copy(dq[i], qw.at[slot], ldq.at[slot])

    def dense_start(s, with_q):
        for i in range(4):
            @pl.when(s // 2 == i)
            def _():
                start_all(dense_load(i, s))
        if with_q:
            for i in range(4):
                @pl.when(jnp.logical_and(s // 2 == i, lax.rem(s, 2) == 0))
                def _():
                    dense_q(i, s).start()

    def send(src, dst, kind, e, dev):
        return pltpu.make_async_remote_copy(src_ref=src, dst_ref=dst, send_sem=remote.at[0, kind, e],
                                            recv_sem=remote.at[1, kind, e], device_id=dev, device_id_type=MESH)

    def send_w(src, dst, kind, i, dev):
        return pltpu.make_async_remote_copy(src_ref=src, dst_ref=dst, send_sem=remote_w.at[0, kind, i],
                                            recv_sem=remote_w.at[1, kind, i], device_id=dev, device_id_type=MESH)

    def r_pk(e, j):
        return send(pk.at[e, j], pk_in.at[e, j], j, e, y_dev)

    def r_pd_c(e):
        return send(pd.at[e, 1 - c], pd_c.at[e], 2, e, c_dev)

    def r_pd_x(e):
        return send(pd.at[e, c], pd_x.at[e], 3, e, x_dev)

    def r_pd_o(e):
        return send(pf.at[e, c], pf.at[e, c], 4, e, c_dev)

    def r_sk_c(e):
        return send(sk.at[e, 1 - c], sk_c.at[e], 5, e, c_dev)

    def r_sk_x(e):
        return send(sk.at[e, c], sk_x.at[e], 6, e, x_dev)

    def r_sk_o(e):
        return send(sf.at[e, c], sf.at[e, c], 7, e, c_dev)

    def r_sd(e):
        return send(sd.at[e], sd_in.at[e], 8, e, y_dev)

    def r_pw(i):
        return send_w(pw.at[i], pw_in.at[i], 0, i, y_dev)

    def r_sw_c(d):
        return send_w(sw.at[2 * d + 1 - c], sw_c.at[d], 1, d, c_dev)

    def r_sw_x(d):
        return send_w(sw.at[2 * d + c], sw_x.at[d], 2, d, x_dev)

    def r_sw_o(d):
        return send_w(sfw.at[2 * d + c], sfw.at[2 * d + c], 3, d, c_dev)

    def out_pk(e):
        return pltpu.make_async_copy(pk_in.at[e], o_pk.at[e], out_sem.at[0, e])

    def out_pf(e):
        return pltpu.make_async_copy(pf.at[e], o_pf.at[e], out_sem.at[1, e])

    def out_sf(e):
        return pltpu.make_async_copy(sf.at[e], o_sf.at[e], out_sem.at[2, e])

    def out_sd(e):
        return pltpu.make_async_copy(sd_in.at[e], o_sd.at[e], out_sem.at[3, e])

    def out_pw(i):
        return pltpu.make_async_copy(pw_in.at[i], o_pd.at[i], outw_sem.at[0, i])

    def out_sfw(i):
        return pltpu.make_async_copy(sfw.at[i], o_sfd.at[i], outw_sem.at[1, i])

    def block(j):
        if j < 2:
            return mk[j] + gk[j].astype(F32)
        return md[...] + gd[...].astype(F32)

    dense_start(0, True)
    for j in range(3):
        start_all(expert_load(j, 0, True))
    pl.semaphore_wait(bar, 3)

    def dense_one(s, carry):
        slot = lax.rem(s, 2)
        i = s // 2

        @pl.when(s < 7)
        def _():
            dense_start(s + 1, True)
        wait_all(dense_load(0, s))

        @pl.when(slot == 0)
        def _():
            dense_q(0, s).wait()
        b = mw[slot] + gw[slot].astype(F32)
        cols = pl.ds(pl.multiple_of(slot * 256, 256), 256)
        pw[i, :, cols] = dot6(qw[lax.rem(i, 2)].T, b, NT)

        @pl.when(slot == 1)
        def _():
            r_pw(i).start()
        return carry

    lax.fori_loop(0, 8, dense_one, 0)

    def pd_mid(e):
        r_pd_c(e).wait_recv()
        pd[e, c] = pd[e, c] + pd_c[e]
        r_pd_x(e).start()

    def expert_one(e, carry):
        for j in range(3):
            wait_all(expert_load(j, e, True))
            q = qk[j] if j < 2 else qd[...]
            part = dot6(q, block(j), NN)

            @pl.when(e < 7)
            def _(j=j):
                start_all(expert_load(j, e + 1, True))
            if j < 2:
                pk[e, j] = part
                r_pk(e, j).start()
            else:
                pd[e, 0] = part[:, :512]
                pd[e, 1] = part[:, 512:]
                r_pd_c(e).start()

        @pl.when(e > 0)
        def _():
            pd_mid(e - 1)
        return carry

    lax.fori_loop(0, 8, expert_one, 0)
    dense_start(0, False)
    for j in range(3):
        start_all(expert_load(j, 0, False))
    pd_mid(7)

    def dense_two(s, carry):
        slot = lax.rem(s, 2)
        i = s // 2

        @pl.when(s < 7)
        def _():
            dense_start(s + 1, False)

        @pl.when(slot == 0)
        def _():
            r_pw(i).wait_recv()
            total = pw[i] + pw_in[i]
            pw_in[i] = total
            out_pw(i).start()
            sw[i, :, 1024:] = dot6(total, total, NT)
            sw[i, :, :1024] = jnp.zeros((128, 1024), F32)
        wait_all(dense_load(0, s))
        b = mw[slot] + gw[slot].astype(F32)
        cols = pl.ds(pl.multiple_of(slot * 256, 256), 256)
        sw[i, :, :1024] = sw[i, :, :1024] + dot6(pw_in[i, :, cols], b, NN)

        @pl.when(lax.rem(s, 4) == 3)
        def _():
            r_sw_c(s // 4).start()
        return carry

    lax.fori_loop(0, 8, dense_two, 0)
    for d in range(2):
        r_sw_c(d).wait_recv()
        sw[2 * d + c] = sw[2 * d + c] + sw_c[d]
        r_sw_x(d).start()

    def sk_mid(e):
        r_sk_c(e).wait_recv()
        sk[e, c] = sk[e, c] + sk_c[e]
        r_sk_x(e).start()

    def expert_two(e, carry):
        r_pd_x(e).wait_recv()
        pf[e, c] = pd[e, c] + pd_x[e]
        r_pd_o(e).start()
        for j in range(2):
            r_pk(e, j).wait_recv()
            total = pk[e, j] + pk_in[e, j]
            pk_in[e, j] = total
            wait_all(expert_load(j, e, False))
            sk[e, j, :, 768:] = dot6(total, rows_to(total, 128), NT)
            sk[e, j, :, :768] = dot6(total, rows_to(block(j), 768), NT)

            @pl.when(e < 7)
            def _(j=j):
                start_all(expert_load(j, e + 1, False))
        out_pk(e).start()
        r_sk_c(e).start()
        r_pd_o(e).wait_recv()
        out_pf(e).start()
        wait_all(expert_load(2, e, False))
        total = jnp.concatenate([pf[e, 0], pf[e, 1]], axis=1)
        sd[e, :, 384:] = dot6(total, rows_to(total, 128), NT)
        sd[e, :, :384] = dot6(total, rows_to(block(2), 384), NT)

        @pl.when(e < 7)
        def _():
            start_all(expert_load(2, e + 1, False))
        r_sd(e).start()
        sk_mid(e)
        return carry

    lax.fori_loop(0, 8, expert_two, 0)

    for d in range(2):
        r_sw_x(d).wait_recv()
        sfw[2 * d + c] = sw[2 * d + c] + sw_x[d]
        r_sw_o(d).start()
    for d in range(2):
        r_sw_o(d).wait_recv()
        out_sfw(2 * d).start()
        out_sfw(2 * d + 1).start()

    def finish_keep(e, carry):
        r_sk_x(e).wait_recv()
        sf[e, c] = sk[e, c] + sk_x[e]
        r_sk_o(e).start()
        return carry

    lax.fori_loop(0, 8, finish_keep, 0)

    def finish(e, carry):
        r_sk_o(e).wait_recv()
        out_sf(e).start()
        r_sd(e).wait_recv()
        sd_in[e] = sd[e] + sd_in[e]
        out_sd(e).start()
        return carry

    lax.fori_loop(0, 8, finish, 0)

    def drain(e, carry):
        for r in (r_pk(e, 0), r_pk(e, 1), r_pd_c(e), r_pd_x(e), r_pd_o(e), r_sk_c(e), r_sk_x(e), r_sk_o(e), r_sd(e)):
            r.wait_send()
        for o in (out_pk(e), out_pf(e), out_sf(e), out_sd(e)):
            o.wait()
        return carry

    lax.fori_loop(0, 8, drain, 0)
    for i in range(4):
        r_pw(i).wait_send()
        out_pw(i).wait()
        out_sfw(i).wait()
    for d in range(2):
        r_sw_c(d).wait_send()
        r_sw_x(d).wait_send()
        r_sw_o(d).wait_send()


def exchange(experts, dense):
    any_spec = pl.BlockSpec(memory_space=pl.ANY)
    args = [a for grp in experts for a in grp] + [a for grp in dense for a in grp]
    shapes = [(8, 2, 88, 512), (8, 2, 88, 512), (8, 2, 88, 896), (8, 88, 512), (4, 128, 512), (4, 128, 1152)]
    dma = pltpu.SemaphoreType.DMA

    def v(*shape, dtype=F32):
        return pltpu.VMEM(shape, dtype)

    scratch = [v(2, 704, 512), v(2, 704, 512, dtype=BF), v(2, 88, 704),
               v(352, 1024), v(352, 1024, dtype=BF), v(88, 352),
               v(2, 256, 1024), v(2, 256, 1024, dtype=BF), v(2, 1024, 128),
               v(8, 2, 88, 512), v(8, 2, 88, 512),
               v(8, 2, 88, 512), v(8, 88, 512), v(8, 88, 512), v(8, 2, 88, 512),
               v(8, 2, 88, 896), v(8, 88, 896), v(8, 88, 896), v(8, 2, 88, 896),
               v(8, 88, 512), v(8, 88, 512),
               v(4, 128, 512), v(4, 128, 512), v(4, 128, 1152), v(2, 128, 1152), v(2, 128, 1152), v(4, 128, 1152),
               dma((3, 3)), dma((2, 2)), dma((2,)), dma((4, 8)), dma((2, 4)), dma((2, 9, 8)), dma((2, 4, 4))]
    return pl.pallas_call(
        exchange_kernel,
        in_specs=[any_spec] * len(args), out_specs=[any_spec] * len(shapes),
        out_shape=[jax.ShapeDtypeStruct(s, F32) for s in shapes],
        scratch_shapes=scratch,
        compiler_params=pltpu.CompilerParams(collective_id=0, has_side_effects=True, vmem_limit_bytes=67043328),
        name='exchange',
    )(*args)


def eliminate(a_ref, li_ref, rank):
    lane = lax.broadcasted_iota(jnp.int32, (8, LANES), 1)
    for k0 in range(0, rank, 8):
        def step(kk, carry, k0=k0):
            k = k0 + kk
            row = a_ref[k]
            at_k = lane == k
            idx = jnp.full((8, LANES), k, jnp.int32)
            piv = jnp.take_along_axis(row, idx, axis=1)
            rinv = 1.0 / piv
            scaled = jnp.where(at_k, rinv, row * rinv)
            rs = 1.0 / jnp.sqrt(piv)
            li_ref[k] = jnp.where(at_k, rs, jnp.where(lane < k, row * rs, 0.0))
            for i in range(k0 + 1, rank):
                cur = a_ref[i]
                g = jnp.take_along_axis(cur, idx, axis=1)
                new = jnp.where(at_k, 0.0, cur) - g * scaled
                if i < k0 + 8:
                    new = jnp.where(i > k, new, cur)
                a_ref[i] = new
            return carry
        lax.fori_loop(0, 8, step, 0)


def factor_kernel(sf_ref, sd_ref, sw_ref, le_ref, lw_ref, rk_ref, rd_ref, rw_ref, nrm,
                  ae, aw, li, lw):
    for e in range(8):
        for j in range(2):
            ae[j, :, e, :] = sf_ref[e, j, :, 768:]
        ae[2, :, e, :] = sd_ref[e, :, 384:]
        aw[:, e, :] = sw_ref[e % 4, :, 1024:]
    for g in range(3):
        eliminate(ae.at[g], li.at[g], 88)
    eliminate(aw, lw, 128)
    lane = lax.broadcasted_iota(jnp.int32, (128, LANES), 1)
    nrm[...] = jnp.zeros((128, LANES), F32)

    def add_norm(rt, where):
        sq = rows_to(jnp.sum(rt * rt, axis=1, keepdims=True), 128)
        nrm[...] = jnp.where(lane == where, sq, nrm[...])

    for e in range(8):
        for j in range(3):
            inv = li[j, :, e, :]
            le_ref[e, j] = inv
            st = sf_ref[e, j, :, :768] if j < 2 else sd_ref[e, :, :384]
            rt = dot6(inv, rows_to(st, 128), NN)
            if j < 2:
                rk_ref[e, j] = rt
            else:
                rd_ref[e] = rt
            add_norm(rt, 8 * j + e)
    for i in range(4):
        inv = lw[:, i, :]
        lw_ref[i] = inv
        rt = dot6(inv, sw_ref[i, :, :1024], NN)
        rw_ref[i] = rt
        add_norm(rt, 24 + i)

def norm_kernel(nrm, dinv_ref, nrm_y, nrm_f, sems):
    t = lax.axis_index('tp')
    f = lax.axis_index('fsdp')
    bar = pltpu.get_barrier_semaphore()
    y_dev = {'tp': 1 - t}
    pl.semaphore_signal(bar, inc=1, device_id=y_dev, device_id_type=MESH)
    for k in range(1, 4):
        pl.semaphore_signal(bar, inc=1, device_id={'fsdp': lax.rem(f + k, 4)}, device_id_type=MESH)
    pl.semaphore_wait(bar, 4)
    copies = [pltpu.make_async_remote_copy(src_ref=nrm, dst_ref=nrm_y, send_sem=sems.at[0, 0], recv_sem=sems.at[1, 0],
                                           device_id=y_dev, device_id_type=MESH)]
    for k in range(1, 4):
        copies.append(pltpu.make_async_remote_copy(src_ref=nrm, dst_ref=nrm_f.at[k], send_sem=sems.at[0, k], recv_sem=sems.at[1, k],
                                                   device_id={'fsdp': lax.rem(f + k, 4)}, device_id_type=MESH))
    for cp in copies:
        cp.start()
    for cp in copies:
        cp.wait()
    own = nrm[...]
    over_f = jnp.zeros((128, LANES), F32)
    for dev in range(4):
        k = lax.rem(f - dev + 4, 4)
        term = jnp.where(k == 0, own, jnp.where(k == 1, nrm_f[1], jnp.where(k == 2, nrm_f[2], nrm_f[3])))
        over_f = over_f + term
    lane = lax.broadcasted_iota(jnp.int32, (128, LANES), 1)
    is_down = jnp.logical_and(lane >= 16, lane < 24)
    total = jnp.where(is_down, over_f, own + nrm_y[...])
    dinv_ref[...] = 1.0 / jnp.sqrt(total)


def factor(sf, sd, sw):
    shapes = [(8, 3, 88, 128), (4, 128, 128), (8, 2, 88, 768), (8, 88, 384), (4, 128, 1024), (128, 128)]
    def v(*shape):
        return pltpu.VMEM(shape, F32)

    spec = pl.BlockSpec(memory_space=pltpu.VMEM)
    return pl.pallas_call(
        factor_kernel, in_specs=[spec] * 3, out_specs=[spec] * 6,
        out_shape=[jax.ShapeDtypeStruct(s, F32) for s in shapes],
        scratch_shapes=[v(3, 88, 8, 128), v(128, 8, 128), v(3, 88, 8, 128), v(128, 8, 128)],
        compiler_params=pltpu.CompilerParams(vmem_limit_bytes=60 * MIB),
        name='factor',
    )(sf, sd, sw)


def norms(nrm):
    spec = pl.BlockSpec(memory_space=pltpu.VMEM)
    return pl.pallas_call(
        norm_kernel, in_specs=[spec], out_specs=spec, out_shape=jax.ShapeDtypeStruct((128, 128), F32),
        scratch_shapes=[pltpu.VMEM((128, 128), F32), pltpu.VMEM((4, 128, 128), F32), pltpu.SemaphoreType.DMA((2, 4))],
        compiler_params=pltpu.CompilerParams(collective_id=1, has_side_effects=True),
        name='norms',
    )(nrm)


def left_cat(ut):
    h, m, l = split3(rows_to(ut, LANES).T)
    return jnp.concatenate([h, l, m, m, h, h], axis=1)


def right_cat(vt):
    h, m, l = split3(rows_to(vt, LANES))
    return jnp.concatenate([l, h, m, h, m, h], axis=0)


def take_col(dinv_ref, rank, where):
    lane = lax.broadcasted_iota(jnp.int32, (rank, LANES), 1)
    return jnp.sum(jnp.where(lane == where, dinv_ref[:rank, :], 0.0), axis=1, keepdims=True)


def apply_update(x_ref, m_ref, g_ref, ut, vt, dinv, x_out, m_out, scale):
    left = left_cat(ut)
    b = m_ref[...] + g_ref[...].astype(F32)
    m_out[...] = b - (1.0 - MOMENTUM) * jnp.dot(left, right_cat(vt), preferred_element_type=F32)
    x_out[...] = x_ref[...] - scale * jnp.dot(left, right_cat(vt * dinv), preferred_element_type=F32)


def expert_kernel(*refs):
    e = pl.program_id(0)
    pk, pf, le, rk, rd, dinv_ref = refs[9:15]
    scale = LEARN_RATE * math.sqrt(2048 / 1408)
    for j in range(3):
        x_ref, m_ref, g_ref = (r.at[0] for r in refs[3 * j:3 * j + 3])
        x_out, m_out, q_out = (r.at[0] for r in refs[15 + 3 * j:18 + 3 * j])
        dinv = take_col(dinv_ref, 88, 8 * j + e)
        if j < 2:
            pt, rt = pk[0, j], rk[0, j, :, :704]
        else:
            pt, rt = jnp.concatenate([pf[0, 0], pf[0, 1]], axis=1), rd[0, :, :352]
        pt = dot6(le[0, j], rows_to(pt, LANES), NN)
        apply_update(x_ref, m_ref, g_ref, rt, pt, dinv, x_out, m_out, scale)
        q_out[...] = rt * dinv


def expert_update(mats, sums):
    def blk(a):
        n = len(a.shape)
        return pl.BlockSpec((1,) + a.shape[1:], lambda e: (e,) + (0,) * (n - 1))

    args = [a for grp in mats for a in grp] + list(sums)
    in_specs = [blk(a) for a in args[:-1]] + [pl.BlockSpec((128, 128), lambda e: (0, 0))]
    out_shape = []
    for x, _, _ in mats:
        q_shape = (8, 88, x.shape[1])
        out_shape += [jax.ShapeDtypeStruct(s, F32) for s in (x.shape, x.shape, q_shape)]
    return pl.pallas_call(
        expert_kernel, grid=(8,), in_specs=in_specs, out_specs=[blk(o) for o in out_shape], out_shape=out_shape,
        compiler_params=pltpu.CompilerParams(vmem_limit_bytes=62 * MIB),
        name='expert_update',
    )(*args)


DENSE_STEPS = 4


def dense_kernel(*refs):
    pw, lw, rw, dinv_ref = refs[12:16]
    part = pl.program_id(0)
    for i in range(4):
        x_ref, m_ref, g_ref = refs[3 * i:3 * i + 3]
        x_out, m_out, q_out = refs[16 + 3 * i:19 + 3 * i]
        dinv = take_col(dinv_ref, 128, 24 + i)
        pt = dot6(lw[i], pw[i], NN)
        apply_update(x_ref, m_ref, g_ref, pt, rw[i], dinv, x_out, m_out, LEARN_RATE)
        q_rows = q_out.shape[0]
        q_out[...] = (rw[i, :, pl.ds(pl.multiple_of(part * q_rows, q_rows), q_rows)] * dinv).T


def dense_update(mats, pw, lw, rw, dinv):
    args = [a for grp in mats for a in grp] + [pw, lw, rw, dinv]
    rows, cols = mats[0][0].shape
    blk = pl.BlockSpec((rows // DENSE_STEPS, cols), lambda s: (s, 0))
    q_blk = pl.BlockSpec((cols // DENSE_STEPS, 128), lambda s: (s, 0))
    in_specs = [blk] * 12 + [pl.BlockSpec((4, 128, rows // DENSE_STEPS), lambda s: (0, 0, s)),
                             pl.BlockSpec(lw.shape, lambda s: (0, 0, 0)),
                             pl.BlockSpec(rw.shape, lambda s: (0, 0, 0)),
                             pl.BlockSpec(dinv.shape, lambda s: (0, 0))]
    w_out = jax.ShapeDtypeStruct((rows, cols), F32)
    return pl.pallas_call(
        dense_kernel, grid=(DENSE_STEPS,), in_specs=in_specs, out_specs=[blk, blk, q_blk] * 4,
        out_shape=[w_out, w_out, jax.ShapeDtypeStruct((cols, 128), F32)] * 4,
        compiler_params=pltpu.CompilerParams(vmem_limit_bytes=60 * MIB),
        name='dense_update',
    )(*args)


def solution(mesh):
    dense_w = P(('layer', 'fsdp'), 'tp')
    dense_f = P(('layer', 'tp'), None)
    stack_w = P('layer', 'fsdp', 'tp')
    stack_f = P('layer', 'tp', None)
    down_f = P('layer', 'fsdp', None)
    in_specs = (dense_w, dense_w, dense_w, dense_f) * 4 + (stack_w, stack_w, stack_w, stack_f) * 2 + (stack_w, stack_w, stack_w, down_f)
    out_specs = (dense_w, dense_w, dense_f) * 4 + (stack_w, stack_w, stack_f) * 2 + (stack_w, stack_w, down_f)

    def local_step(*blocks):
        dense = [blocks[4 * i:4 * i + 4] for i in range(4)]
        experts = []
        for i in (4, 5, 6):
            w, m, g, q = blocks[4 * i:4 * i + 4]
            if i < 6:
                w, m, g = (a.swapaxes(1, 2) for a in (w, m, g))
            experts.append((w, m, g, q.swapaxes(1, 2)))
        pk, pf, sf, sd, pw, sfw = exchange([grp[1:] for grp in experts], [grp[1:] for grp in dense])
        le, lw, rk, rd, rw, nrm = factor(sf, sd, sfw)
        dinv = norms(nrm)
        results = list(dense_update([grp[:3] for grp in dense], pw, lw, rw, dinv))
        out = list(expert_update([grp[:3] for grp in experts], (pk, pf, le, rk, rd, dinv)))
        for n in range(9):
            if n < 6 or n == 8:
                out[n] = out[n].swapaxes(1, 2)
        return tuple(results + out)

    return jax.shard_map(local_step, mesh=mesh, in_specs=in_specs, out_specs=out_specs, check_vma=False)
```

time: 1040 us -> 290 us (0.28)
  other arithmetic: 472 us -> 0 us
  Pallas kernels: 0 us -> 288 us
  matrix products: 284 us -> 0 us
  waiting for transfers between devices: 234 us -> 0 us
  local copies, waits for them, and re-layouts: 15.6 us -> 0 us
  blocking collectives: 14.5 us -> 0 us
  between operations: 15.1 us -> 0.86 us
    another operation x37 -> x0, other arithmetic: 456 us -> none  [the longest x20 250 us: dion_local(): chol_low = jnp.linalg.cholesky(gram_mat)]
    pallas_call x0 -> x5, Pallas kernels: none -> 288 us  [the longest x1 135 us: exchange(): pl.pallas_call(exchange_kernel, in_specs=[any_spec] * len(args), out_spec...]
    dot_general x35 -> x0, matrix products: 270 us -> none  [mat_mul(): jnp.einsum(form, left_op, right_op, preferred_element_type=jnp.float32, p...]
    psum x5 -> x0, waiting for transfers between devices: 234 us -> none  [the longest x1 86.3 us: dion_local(): p_tilde = lax.psum(mat_mul(forms[0], mom_grad, factor), short_axis)]
    psum x2 -> x0, blocking collectives: 14.5 us -> none  [dion_local(): col_sq = lax.psum(jnp.sum(r_new * r_new, axis=1, keepdims=True), short_axis)]
    another operation x7 -> x0, matrix products: 14.5 us -> none  [dion_local(): lax.linalg.triangular_solve(chol_low, p_tilde, left_side=False, lower=Tru...]
  transfers between devices with their start and end apart: 5 -> 0, of which waited for: 3 -> 0; matrix products, arithmetic and copies ran while one was open for 31% -> 0% of each run, Pallas kernels for 0% -> 0%
where the time goes in v2:
time: 290 us; the launch traced here: 289 us
  Pallas kernels  288 us (99%)
    pallas_call x1, Pallas kernels, exchange(): pl.pallas_call(exchange_kernel, in_specs=[any_spec] * len(args), out_spec...  135 us
    pallas_call x1, Pallas kernels, factor(): pl.pallas_call(factor_kernel, in_specs=[spec] * 3, out_specs=[spec] * 6,...  65.5 us
    pallas_call x1, Pallas kernels, expert_update(): pl.pallas_call(expert_kernel, grid=(8,), in_specs=in_specs, out_specs=[bl...  61.9 us
    pallas_call x1, Pallas kernels, dense_update(): pl.pallas_call(dense_kernel, grid=(DENSE_STEPS,), in_specs=in_specs, out_...  19.2 us
    pallas_call x1, Pallas kernels, norms(): pl.pallas_call(norm_kernel, in_specs=[spec], out_specs=spec, out_shape=ja...  6.59 us

profile of v2, /device:TPU:0, one launch (start us, length us, event | category | flops | bytes accessed | tf_op | source)
XLA Modules:
  0.0 289.3 jit_solution(13787377032390040148)
XLA Ops:
  0.7 135.3 %exchange.1 = (f32[8,2,88,512]{3,2,1,0:T(8,128)}, f32[8,2,88,512]{3,2,1,0:T(8,128)}, f32[8,2,88,896]{3,2,1,0:T(8,128)}, f32[8,88,512]{2,1,0:T(8,128)}, f32[4,128,512]{2,1,0:T(8,128)}, /*index=5*/f32[4,128,1152]{2,1,0:T(8,128)}) custom-call(f32[8,704,512]{2,1,0:T(8,128)} %bitcast.16, bf16[8,704,512]{2,1,0:T(8,128)(2,1)} %bitcast.20, f32[8,88,704]{2,1,0:T(8,128)} %bitcast.26, ...), custom_call_target="tpu_custom_call" | custom-call | tf_op jit(solution)/shard_map/exchange/pallas_call | solution.py:364
  135.9 65.5 %factor.1 = (f32[8,3,88,128]{3,2,1,0:T(8,128)}, f32[4,128,128]{2,1,0:T(8,128)}, f32[8,2,88,768]{3,2,1,0:T(8,128)}, f32[8,88,384]{2,1,0:T(8,128)}, f32[4,128,1024]{2,1,0:T(8,128)}, /*index=5*/f32[128,128]{1,0:T(8,128)}) custom-call(f32[8,2,88,896]{3,2,1,0:T(8,128)} %get-tuple-element.55.sf_ref, f32[8,88,512]{2,1,0:T(8,128)} %get-tuple-element.56.sd_ref, ...), custom_call_target="tpu_custom_call" | custom-call | tf_op jit(solution)/shard_map/factor/pallas_call | solution.py:469
  201.4 6.6 %norms.1.refs_15_.refs_14_ = f32[128,128]{1,0:T(8,128)} custom-call(f32[128,128]{1,0:T(8,128)} %get-tuple-element.60.nrm), custom_call_target="tpu_custom_call" | custom-call | tf_op jit(solution)/shard_map/norms/pallas_call | solution.py:480
  208.0 61.9 %expert_update.1 = (f32[8,704,512]{2,1,0:T(8,128)}, f32[8,704,512]{2,1,0:T(8,128)}, f32[8,88,704]{2,1,0:T(8,128)}, f32[8,704,512]{2,1,0:T(8,128)}, f32[8,704,512...) custom-call(f32[8,704,512]{2,1,0:T(8,128)} %bitcast.24, ...), custom_call_target="tpu_custom_call" | custom-call | tf_op jit(solution)/shard_map/expert_update/pallas_call | solution.py:538
  269.9 19.2 %dense_update.1 = (f32[512,1024]{1,0:T(8,128)}, f32[512,1024]{1,0:T(8,128)}, f32[1024,128]{1,0:T(8,128)}, f32[512,1024]{1,0:T(8,128)}, f32[512,1024]{1,0:T(8,128...) custom-call(f32[512,1024]{1,0:T(8,128)} %refs_0_.1, ...), custom_call_target="tpu_custom_call" | custom-call | tf_op jit(solution)/shard_map/dense_update/pallas_call | solution.py:571

commit v3 on v2

v3 whole, which is shorter than its diff:
```python
import math
import jax
import jax.numpy as jnp
from jax import lax
from jax.experimental import pallas as pl
from jax.experimental.pallas import tpu as pltpu
from jax.sharding import PartitionSpec as P

MOMENTUM = 0.9
LEARN_RATE = 0.3
LANES = 128
BF = jnp.bfloat16
F32 = jnp.float32
MIB = 2 ** 20
NN = (((1,), (0,)), ((), ()))
NT = (((1,), (1,)), ((), ()))
MESH = pl.DeviceIdType.MESH


def split3(x):
    hi = x.astype(BF)
    rest = x - hi.astype(F32)
    mid = rest.astype(BF)
    low = (rest - mid.astype(F32)).astype(BF)
    return hi, mid, low


def rows_to(x, rows):
    have, cols = x.shape
    if have == rows:
        return x
    return jnp.concatenate([x, jnp.zeros((rows - have, cols), x.dtype)], axis=0)


def dot6(left, right, dims):
    rank = left.shape[0]
    pad = -(-rank // 16) * 16
    lh, lm, ll = split3(rows_to(left, pad))
    rh, rm, rl = split3(right)
    with_h = lax.dot_general(jnp.concatenate([lh, lm, ll], axis=0), rh, dims, preferred_element_type=F32)
    with_m = lax.dot_general(jnp.concatenate([lh, lm], axis=0), rm, dims, preferred_element_type=F32)
    with_l = lax.dot_general(lh, rl, dims, preferred_element_type=F32)
    small = with_h[2 * pad:2 * pad + rank] + with_m[pad:pad + rank] + with_l[:rank]
    mid = with_h[pad:pad + rank] + with_m[:rank]
    return (small + mid) + with_h[:rank]


def eliminate(a, li, rank):
    lane = lax.broadcasted_iota(jnp.int32, (8, LANES), 1)

    def pick(x, hit):
        return jnp.sum(jnp.where(hit, x, 0.0), axis=-1, keepdims=True)

    for k0 in range(0, rank, 8):
        def step(kk, carry, k0=k0):
            k = k0 + 2 * kk
            h0, h1 = lane == k, lane == k + 1
            r0, r1 = a[k], a[k + 1]
            v00, v01, v10, v11 = pick(r0, h0), pick(r0, h1), pick(r1, h0), pick(r1, h1)
            rinv0 = 1.0 / v00
            rs0 = 1.0 / jnp.sqrt(v00)
            s01 = v01 * rinv0
            sc0 = jnp.where(h0, rinv0, r0 * rinv0)
            li[k] = jnp.where(h0, rs0, jnp.where(lane < k, r0 * rs0, 0.0))
            piv1 = v11 - v10 * s01
            rinv1 = 1.0 / piv1
            rs1 = 1.0 / jnp.sqrt(piv1)
            r1 = jnp.where(h0, 0.0, r1) - v10 * sc0
            sc1 = jnp.where(h1, rinv1, r1 * rinv1)
            li[k + 1] = jnp.where(h1, rs1, jnp.where(lane < k + 1, r1 * rs1, 0.0))
            sc0 = jnp.where(h1, 0.0, sc0)

            def below(lo, n, masked):
                lane_n = lax.broadcasted_iota(jnp.int32, (n, 8, LANES), 2)
                g_hit0, g_hit1 = lane_n == k, lane_n == k + 1
                cur = a[lo:lo + n]
                g0 = pick(cur, g_hit0)
                g1 = pick(cur, g_hit1) - g0 * s01[None]
                new = jnp.where(jnp.logical_or(g_hit0, g_hit1), 0.0, cur) - g0 * sc0[None] - g1 * sc1[None]
                if masked:
                    row = lo + lax.broadcasted_iota(jnp.int32, (n, 8, LANES), 0)
                    new = jnp.where(row > k + 1, new, cur)
                a[lo:lo + n] = new

            below(k0, 8, True)
            if rank > k0 + 8:
                below(k0 + 8, rank - k0 - 8, False)
            return carry
        lax.fori_loop(0, 4, step, 0)


def exchange_kernel(*refs):
    em, eg, eq = refs[0:9:3], refs[1:9:3], refs[2:9:3]
    dm, dg, dq = refs[9:21:3], refs[10:21:3], refs[11:21:3]
    o_pk, o_pf, o_sf, o_sd, o_pd, o_sfd, o_nrm = refs[21:28]
    (mk, gk, qk, md, gd, qd, mw, gw, qw,
     pk, pk_in, pd, pd_c, pd_x, pf, sk, sk_c, sk_x, sf, sd, sd_in, wd, wd_in,
     pw, pw_in, sw, sw_c, sw_x, sfw, ae, li, aw, lw, nrm, nrm_y, nrm_d, nrm_f,
     ld, ldw, ldq, out_sem, outw_sem, remote, remote_w, remote_n) = refs[28:]
    t = lax.axis_index('tp')
    f = lax.axis_index('fsdp')
    c = lax.rem(f, 2)
    y_dev = {'tp': 1 - t}
    c_dev = {'fsdp': f + 1 - 2 * c}
    x_dev = {'fsdp': lax.rem(f + 2, 4)}
    xc_dev = {'fsdp': lax.rem(f + 3 - 2 * c, 4)}
    yc_dev = {'tp': 1 - t, 'fsdp': f + 1 - 2 * c}
    bar = pltpu.get_barrier_semaphore()
    for dev in (y_dev, c_dev, x_dev, xc_dev, yc_dev):
        pl.semaphore_signal(bar, inc=1, device_id=dev, device_id_type=MESH)

    def expert_load(j, e, with_q):
        m_buf, g_buf, q_buf = (mk.at[j], gk.at[j], qk.at[j]) if j < 2 else (md, gd, qd)
        copies = [pltpu.make_async_copy(em[j].at[e], m_buf, ld.at[j, 0]),
                  pltpu.make_async_copy(eg[j].at[e], g_buf, ld.at[j, 1])]
        if with_q:
            copies.append(pltpu.make_async_copy(eq[j].at[e], q_buf, ld.at[j, 2]))
        return copies

    def start_all(copies):
        for cp in copies:
            cp.start()

    def wait_all(copies):
        for cp in copies:
            cp.wait()

    def dense_load(i, s):
        slot = lax.rem(s, 2)
        rows = pl.ds(pl.multiple_of(slot * 256, 256), 256)
        return [pltpu.make_async_copy(dm[i].at[rows], mw.at[slot], ldw.at[slot, 0]),
                pltpu.make_async_copy(dg[i].at[rows], gw.at[slot], ldw.at[slot, 1])]

    def dense_q(i, s):
        slot = lax.rem(s // 2, 2)
        return pltpu.make_async_copy(dq[i], qw.at[slot], ldq.at[slot])

    def dense_start(s, with_q):
        for i in range(4):
            @pl.when(s // 2 == i)
            def _():
                start_all(dense_load(i, s))
        if with_q:
            for i in range(4):
                @pl.when(jnp.logical_and(s // 2 == i, lax.rem(s, 2) == 0))
                def _():
                    dense_q(i, s).start()

    def send(src, dst, kind, e, dev):
        return pltpu.make_async_remote_copy(src_ref=src, dst_ref=dst, send_sem=remote.at[0, kind, e],
                                            recv_sem=remote.at[1, kind, e], device_id=dev, device_id_type=MESH)

    def send_w(src, dst, kind, i, dev):
        return pltpu.make_async_remote_copy(src_ref=src, dst_ref=dst, send_sem=remote_w.at[0, kind, i],
                                            recv_sem=remote_w.at[1, kind, i], device_id=dev, device_id_type=MESH)

    def send_n(dst, kind, dev):
        return pltpu.make_async_remote_copy(src_ref=nrm, dst_ref=dst, send_sem=remote_n.at[0, kind],
                                            recv_sem=remote_n.at[1, kind], device_id=dev, device_id_type=MESH)

    def r_pk(e, j):
        return send(pk.at[e, j], pk_in.at[e, j], j, e, y_dev)

    def r_pd_c(e):
        return send(pd.at[e, 1 - c], pd_c.at[e], 2, e, c_dev)

    def r_pd_x(e):
        return send(pd.at[e, c], pd_x.at[e], 3, e, x_dev)

    def r_pd_o(e):
        return send(pf.at[e, c], pf.at[e, c], 4, e, c_dev)

    def r_sk_c(e):
        return send(sk.at[e, 1 - c], sk_c.at[e], 5, e, c_dev)

    def r_sk_x(e):
        return send(sk.at[e, c], sk_x.at[e], 6, e, x_dev)

    def r_sk_o(e):
        return send(sf.at[e, c], sf.at[e, c], 7, e, c_dev)

    def r_sd(e):
        return send(sd.at[e], sd_in.at[e, :, 0:384], 8, e, y_dev)

    def r_wd(e):
        return send(wd.at[e], wd_in.at[e], 9, e, y_dev)

    def r_pw(i):
        return send_w(pw.at[i], pw_in.at[i], 0, i, y_dev)

    def r_sw_c(d):
        return send_w(sw.at[2 * d + 1 - c], sw_c.at[d], 1, d, c_dev)

    def r_sw_x(d):
        return send_w(sw.at[2 * d + c], sw_x.at[d], 2, d, x_dev)

    def r_sw_o(d):
        return send_w(sfw.at[2 * d + c], sfw.at[2 * d + c], 3, d, c_dev)

    def out_pk(e):
        return pltpu.make_async_copy(pk_in.at[e], o_pk.at[e], out_sem.at[0, e])

    def out_pf(e):
        return pltpu.make_async_copy(pf.at[e], o_pf.at[e], out_sem.at[1, e])

    def out_sf(e, j):
        return pltpu.make_async_copy(sf.at[e, j], o_sf.at[e, j], out_sem.at[2 + j, e])

    def out_sd(e):
        return pltpu.make_async_copy(sd_in.at[e], o_sd.at[e], out_sem.at[4, e])

    def out_pw(i):
        return pltpu.make_async_copy(pw_in.at[i], o_pd.at[i], outw_sem.at[0, i])

    def out_sfw(i):
        return pltpu.make_async_copy(sfw.at[i], o_sfd.at[i], outw_sem.at[1, i])

    def block(j):
        if j < 2:
            return mk[j] + gk[j].astype(F32)
        return md[...] + gd[...].astype(F32)

    dense_start(0, True)
    for j in range(3):
        start_all(expert_load(j, 0, True))
    pl.semaphore_wait(bar, 5)

    def dense_one(s, carry):
        slot = lax.rem(s, 2)
        i = s // 2

        @pl.when(s < 7)
        def _():
            dense_start(s + 1, True)
        wait_all(dense_load(0, s))

        @pl.when(slot == 0)
        def _():
            dense_q(0, s).wait()
        b = mw[slot] + gw[slot].astype(F32)
        cols = pl.ds(pl.multiple_of(slot * 256, 256), 256)
        pw[i, :, cols] = dot6(qw[lax.rem(i, 2)].T, b, NT)

        @pl.when(slot == 1)
        def _():
            r_pw(i).start()
        return carry

    lax.fori_loop(0, 8, dense_one, 0)

    def pd_mid(e):
        r_pd_c(e).wait_recv()
        pd[e, c] = pd[e, c] + pd_c[e]
        r_pd_x(e).start()

    def expert_one(e, carry):
        for j in (2, 0, 1):
            wait_all(expert_load(j, e, True))
            q = qk[j] if j < 2 else qd[...]
            part = dot6(q, block(j), NN)

            @pl.when(e < 7)
            def _(j=j):
                start_all(expert_load(j, e + 1, True))
            if j < 2:
                pk[e, j] = part
                r_pk(e, j).start()
            else:
                pd[e, 0] = part[:, :512]
                pd[e, 1] = part[:, 512:]
                r_pd_c(e).start()
        pd_mid(e)
        return carry

    lax.fori_loop(0, 8, expert_one, 0)
    dense_start(0, False)
    for j in range(3):
        start_all(expert_load(j, 0, False))

    def dense_two(s, carry):
        slot = lax.rem(s, 2)
        i = s // 2

        @pl.when(s < 7)
        def _():
            dense_start(s + 1, False)

        @pl.when(slot == 0)
        def _():
            r_pw(i).wait_recv()
            total = pw[i] + pw_in[i]
            pw_in[i] = total
            out_pw(i).start()
            sw[i, :, 1024:] = dot6(total, total, NT)
            sw[i, :, :1024] = jnp.zeros((128, 1024), F32)
        wait_all(dense_load(0, s))
        b = mw[slot] + gw[slot].astype(F32)
        cols = pl.ds(pl.multiple_of(slot * 256, 256), 256)
        sw[i, :, :1024] = sw[i, :, :1024] + dot6(pw_in[i, :, cols], b, NN)

        @pl.when(lax.rem(s, 4) == 3)
        def _():
            r_sw_c(s // 4).start()
        return carry

    lax.fori_loop(0, 8, dense_two, 0)
    for d in range(2):
        r_sw_c(d).wait_recv()
        sw[2 * d + c] = sw[2 * d + c] + sw_c[d]
        r_sw_x(d).start()

    def down_two(s, carry):
        @pl.when(s < 8)
        def _():
            r_pd_x(s).wait_recv()
            pf[s, c] = pd[s, c] + pd_x[s]
            r_pd_o(s).start()

        @pl.when(s > 0)
        def _():
            e = s - 1
            r_pd_o(e).wait_recv()
            out_pf(e).start()
            wait_all(expert_load(2, e, False))
            total = jnp.concatenate([pf[e, 0], pf[e, 1]], axis=1)
            wd[e] = dot6(total, rows_to(total, 128), NT)
            r_wd(e).start()
            sd[e] = dot6(total, rows_to(block(2), 384), NT)

            @pl.when(e < 7)
            def _():
                start_all(expert_load(2, e + 1, False))
        return carry

    lax.fori_loop(0, 9, down_two, 0)

    def sd_send(e, carry):
        r_sd(e).start()
        return carry

    lax.fori_loop(0, 8, sd_send, 0)

    def keep_two(e, carry):
        for j in range(2):
            r_pk(e, j).wait_recv()
            total = pk[e, j] + pk_in[e, j]
            pk_in[e, j] = total
            wait_all(expert_load(j, e, False))
            sk[e, j, :, 768:] = dot6(total, rows_to(total, 128), NT)
            sk[e, j, :, :768] = dot6(total, rows_to(block(j), 768), NT)

            @pl.when(e < 7)
            def _(j=j):
                start_all(expert_load(j, e + 1, False))
        r_sk_c(e).start()
        out_pk(e).start()
        r_sk_c(e).wait_recv()
        sk[e, c] = sk[e, c] + sk_c[e]
        r_sk_x(e).start()
        return carry

    nrm[...] = jnp.zeros((128, LANES), F32)
    lane_full = lax.broadcasted_iota(jnp.int32, (128, LANES), 1)

    def add_norm(rt, where):
        sq = rows_to(jnp.sum(rt * rt, axis=1, keepdims=True), 128)
        nrm[...] = jnp.where(lane_full == where, sq, nrm[...])

    lax.fori_loop(0, 4, keep_two, 0)

    for d in range(2):
        r_sw_x(d).wait_recv()
        sfw[2 * d + c] = sw[2 * d + c] + sw_x[d]
    for s in range(8):
        aw[:, s, :] = sfw[2 * (s % 2) + c, :, 1024:]
    eliminate(aw, lw, 128)
    for d in range(2):
        i = 2 * d + c
        inv = lw[:, d, :]
        sfw[i, :, 1024:] = inv
        rt = dot6(inv, sfw[i, :, :1024], NN)
        sfw[i, :, :1024] = rt
        add_norm(rt, 24 + i)
        r_sw_o(d).start()

    lax.fori_loop(4, 8, keep_two, 0)

    for e in range(8):
        r_wd(e).wait_recv()
        ae[:, e, :] = wd[e] + wd_in[e]
    eliminate(ae, li, 88)
    for e in range(8):
        sd_in[e, :, 384:] = li[:, e, :]

    def keep_total(e, carry):
        r_sk_x(e).wait_recv()
        sf[e, c] = sk[e, c] + sk_x[e]
        return carry

    lax.fori_loop(0, 8, keep_total, 0)
    for e in range(8):
        ae[:, e, :] = sf[e, c, :, 768:]
    eliminate(ae, li, 88)
    for e in range(8):
        sf[e, c, :, 768:] = li[:, e, :]

    def keep_r(e, carry):
        rt = dot6(sf[e, c, :, 768:], rows_to(sf[e, c, :, :768], 128), NN)
        sf[e, c, :, :768] = rt
        add_norm(rt, 8 * c + e)
        r_sk_o(e).start()
        out_sf(e, c).start()
        return carry

    lax.fori_loop(0, 8, keep_r, 0)

    def down_r(e, carry):
        r_sd(e).wait_recv()
        st = sd[e] + sd_in[e, :, :384]
        rt = dot6(sd_in[e, :, 384:], rows_to(st, 128), NN)
        sd_in[e, :, :384] = rt
        add_norm(rt, 16 + e)
        out_sd(e).start()
        return carry

    lax.fori_loop(0, 8, down_r, 0)

    copies = [send_n(nrm_y, 0, y_dev), send_n(nrm_d, 1, yc_dev)]
    for k in range(1, 4):
        copies.append(send_n(nrm_f.at[k - 1], k + 1, {'fsdp': lax.rem(f + k, 4)}))
    start_all(copies)

    def finish(e, carry):
        r_sk_o(e).wait_recv()
        out_sf(e, 1 - c).start()
        return carry

    lax.fori_loop(0, 8, finish, 0)
    for d in range(2):
        out_sfw(2 * d + c).start()
        r_sw_o(d).wait_recv()
        out_sfw(2 * d + 1 - c).start()
    wait_all(copies)
    own = nrm[...]
    over_f = jnp.zeros((128, LANES), F32)
    for dev in range(4):
        k = lax.rem(f - dev + 4, 4)
        over_f = over_f + jnp.where(k == 0, own, jnp.where(k == 1, nrm_f[0], jnp.where(k == 2, nrm_f[1], nrm_f[2])))
    core = jnp.where(c == 0, nrm_f[2], nrm_f[0])
    owner = jnp.where(lane_full < 24, lane_full // 8, lax.rem(lane_full, 2))
    keep = jnp.where(owner == c, own + nrm_y[...], core + nrm_d[...])
    is_down = jnp.logical_and(lane_full >= 16, lane_full < 24)
    total = jnp.where(is_down, over_f, keep)
    nrm[...] = 1.0 / jnp.sqrt(total)
    last = pltpu.make_async_copy(nrm, o_nrm, outw_sem.at[0, 4])
    last.start()

    def drain(e, carry):
        for r in (r_pk(e, 0), r_pk(e, 1), r_pd_c(e), r_pd_x(e), r_pd_o(e), r_sk_c(e), r_sk_x(e), r_sk_o(e), r_sd(e), r_wd(e)):
            r.wait_send()
        for o in (out_pk(e), out_pf(e), out_sf(e, 0), out_sf(e, 1), out_sd(e)):
            o.wait()
        return carry

    lax.fori_loop(0, 8, drain, 0)
    for i in range(4):
        r_pw(i).wait_send()
        out_pw(i).wait()
        out_sfw(i).wait()
    for d in range(2):
        r_sw_c(d).wait_send()
        r_sw_x(d).wait_send()
        r_sw_o(d).wait_send()
    last.wait()


def exchange(experts, dense):
    any_spec = pl.BlockSpec(memory_space=pl.ANY)
    args = [a for grp in experts for a in grp] + [a for grp in dense for a in grp]
    shapes = [(8, 2, 88, 512), (8, 2, 88, 512), (8, 2, 88, 896), (8, 88, 512), (4, 128, 512), (4, 128, 1152), (128, 128)]
    dma = pltpu.SemaphoreType.DMA

    def v(*shape, dtype=F32):
        return pltpu.VMEM(shape, dtype)

    scratch = [v(2, 704, 512), v(2, 704, 512, dtype=BF), v(2, 88, 704),
               v(352, 1024), v(352, 1024, dtype=BF), v(88, 352),
               v(2, 256, 1024), v(2, 256, 1024, dtype=BF), v(2, 1024, 128),
               v(8, 2, 88, 512), v(8, 2, 88, 512),
               v(8, 2, 88, 512), v(8, 88, 512), v(8, 88, 512), v(8, 2, 88, 512),
               v(8, 2, 88, 896), v(8, 88, 896), v(8, 88, 896), v(8, 2, 88, 896),
               v(8, 88, 384), v(8, 88, 512), v(8, 88, 128), v(8, 88, 128),
               v(4, 128, 512), v(4, 128, 512), v(4, 128, 1152), v(2, 128, 1152), v(2, 128, 1152), v(4, 128, 1152),
               v(88, 8, 128), v(88, 8, 128), v(128, 8, 128), v(128, 8, 128),
               v(128, 128), v(128, 128), v(128, 128), v(3, 128, 128),
               dma((3, 3)), dma((2, 2)), dma((2,)), dma((5, 8)), dma((2, 5)), dma((2, 10, 8)), dma((2, 4, 4)), dma((2, 5))]
    return pl.pallas_call(
        exchange_kernel,
        in_specs=[any_spec] * len(args), out_specs=[any_spec] * len(shapes),
        out_shape=[jax.ShapeDtypeStruct(s, F32) for s in shapes],
        scratch_shapes=scratch,
        compiler_params=pltpu.CompilerParams(collective_id=0, has_side_effects=True, vmem_limit_bytes=67043328),
        name='exchange',
    )(*args)


def left_cat(ut):
    h, m, l = split3(rows_to(ut, LANES).T)
    return jnp.concatenate([h, l, m, m, h, h], axis=1)


def right_cat(vt):
    h, m, l = split3(rows_to(vt, LANES))
    return jnp.concatenate([l, h, m, h, m, h], axis=0)


def take_col(dinv_ref, rank, where):
    lane = lax.broadcasted_iota(jnp.int32, (rank, LANES), 1)
    return jnp.sum(jnp.where(lane == where, dinv_ref[:rank, :], 0.0), axis=1, keepdims=True)


def apply_update(x_ref, m_ref, g_ref, ut, vt, dinv, x_out, m_out, scale):
    left = left_cat(ut)
    b = m_ref[...] + g_ref[...].astype(F32)
    m_out[...] = b - (1.0 - MOMENTUM) * jnp.dot(left, right_cat(vt), preferred_element_type=F32)
    x_out[...] = x_ref[...] - scale * jnp.dot(left, right_cat(vt * dinv), preferred_element_type=F32)


def expert_kernel(*refs):
    e = pl.program_id(0)
    pk, pf, sf, sd, dinv_ref = refs[9:14]
    scale = LEARN_RATE * math.sqrt(2048 / 1408)
    for j in range(3):
        x_ref, m_ref, g_ref = (r.at[0] for r in refs[3 * j:3 * j + 3])
        x_out, m_out, q_out = (r.at[0] for r in refs[14 + 3 * j:17 + 3 * j])
        dinv = take_col(dinv_ref, 88, 8 * j + e)
        if j < 2:
            pt, rt, inv = pk[0, j], sf[0, j, :, :704], sf[0, j, :, 768:]
        else:
            pt, rt, inv = jnp.concatenate([pf[0, 0], pf[0, 1]], axis=1), sd[0, :, :352], sd[0, :, 384:]
        pt = dot6(inv, rows_to(pt, LANES), NN)
        apply_update(x_ref, m_ref, g_ref, rt, pt, dinv, x_out, m_out, scale)
        q_out[...] = rt * dinv


def expert_update(mats, sums):
    def blk(a):
        n = len(a.shape)
        return pl.BlockSpec((1,) + a.shape[1:], lambda e: (e,) + (0,) * (n - 1))

    args = [a for grp in mats for a in grp] + list(sums)
    in_specs = [blk(a) for a in args[:-1]] + [pl.BlockSpec((128, 128), lambda e: (0, 0))]
    out_shape = []
    for x, _, _ in mats:
        q_shape = (8, 88, x.shape[1])
        out_shape += [jax.ShapeDtypeStruct(s, F32) for s in (x.shape, x.shape, q_shape)]
    return pl.pallas_call(
        expert_kernel, grid=(8,), in_specs=in_specs, out_specs=[blk(o) for o in out_shape], out_shape=out_shape,
        compiler_params=pltpu.CompilerParams(vmem_limit_bytes=62 * MIB),
        name='expert_update',
    )(*args)


DENSE_STEPS = 4


def dense_kernel(*refs):
    pw, sfw, dinv_ref = refs[12:15]
    part = pl.program_id(0)
    for i in range(4):
        x_ref, m_ref, g_ref = refs[3 * i:3 * i + 3]
        x_out, m_out, q_out = refs[15 + 3 * i:18 + 3 * i]
        dinv = take_col(dinv_ref, 128, 24 + i)
        pt = dot6(sfw[i, :, 1024:], pw[i], NN)
        apply_update(x_ref, m_ref, g_ref, pt, sfw[i, :, :1024], dinv, x_out, m_out, LEARN_RATE)
        q_rows = q_out.shape[0]
        q_out[...] = (sfw[i, :, pl.ds(pl.multiple_of(part * q_rows, q_rows), q_rows)] * dinv).T


def dense_update(mats, pw, sfw, dinv):
    args = [a for grp in mats for a in grp] + [pw, sfw, dinv]
    rows, cols = mats[0][0].shape
    blk = pl.BlockSpec((rows // DENSE_STEPS, cols), lambda s: (s, 0))
    q_blk = pl.BlockSpec((cols // DENSE_STEPS, 128), lambda s: (s, 0))
    in_specs = [blk] * 12 + [pl.BlockSpec((4, 128, rows // DENSE_STEPS), lambda s: (0, 0, s)),
                             pl.BlockSpec(sfw.shape, lambda s: (0, 0, 0)),
                             pl.BlockSpec(dinv.shape, lambda s: (0, 0))]
    w_out = jax.ShapeDtypeStruct((rows, cols), F32)
    return pl.pallas_call(
        dense_kernel, grid=(DENSE_STEPS,), in_specs=in_specs, out_specs=[blk, blk, q_blk] * 4,
        out_shape=[w_out, w_out, jax.ShapeDtypeStruct((cols, 128), F32)] * 4,
        compiler_params=pltpu.CompilerParams(vmem_limit_bytes=60 * MIB),
        name='dense_update',
    )(*args)


def solution(mesh):
    dense_w = P(('layer', 'fsdp'), 'tp')
    dense_f = P(('layer', 'tp'), None)
    stack_w = P('layer', 'fsdp', 'tp')
    stack_f = P('layer', 'tp', None)
    down_f = P('layer', 'fsdp', None)
    in_specs = (dense_w, dense_w, dense_w, dense_f) * 4 + (stack_w, stack_w, stack_w, stack_f) * 2 + (stack_w, stack_w, stack_w, down_f)
    out_specs = (dense_w, dense_w, dense_f) * 4 + (stack_w, stack_w, stack_f) * 2 + (stack_w, stack_w, down_f)

    def local_step(*blocks):
        dense = [blocks[4 * i:4 * i + 4] for i in range(4)]
        experts = []
        for i in (4, 5, 6):
            w, m, g, q = blocks[4 * i:4 * i + 4]
            if i < 6:
                w, m, g = (a.swapaxes(1, 2) for a in (w, m, g))
            experts.append((w, m, g, q.swapaxes(1, 2)))
        pk, pf, sf, sd, pw, sfw, dinv = exchange([grp[1:] for grp in experts], [grp[1:] for grp in dense])
        results = list(dense_update([grp[:3] for grp in dense], pw, sfw, dinv))
        out = list(expert_update([grp[:3] for grp in experts], (pk, pf, sf, sd, dinv)))
        for n in range(9):
            if n < 6 or n == 8:
                out[n] = out[n].swapaxes(1, 2)
        return tuple(results + out)

    return jax.shard_map(local_step, mesh=mesh, in_specs=in_specs, out_specs=out_specs, check_vma=False)
```

time: 290 us -> 237 us (0.82)
  Pallas kernels: 288 us -> 236 us
    pallas_call x2 -> x0, Pallas kernels: 72.1 us -> none  [the longest x1 65.5 us: factor(): pl.pallas_call(factor_kernel, in_specs=[spec] * 3, out_specs=[spec] * 6,...]
    pallas_call x1, Pallas kernels: 135 us -> 155 us  [exchange(): pl.pallas_call(exchange_kernel, in_specs=[any_spec] * len(args), out_spec...]
where the time goes in v3:
time: 237 us
  Pallas kernels  236 us (100%)
    pallas_call x1, Pallas kernels, exchange(): pl.pallas_call(exchange_kernel, in_specs=[any_spec] * len(args), out_spec...  155 us
    pallas_call x1, Pallas kernels, expert_update(): pl.pallas_call(expert_kernel, grid=(8,), in_specs=in_specs, out_specs=[bl...  61.9 us
    pallas_call x1, Pallas kernels, dense_update(): pl.pallas_call(dense_kernel, grid=(DENSE_STEPS,), in_specs=in_specs, out_...  19.3 us

profile of v3, /device:TPU:0, one launch (start us, length us, event | category | flops | bytes accessed | tf_op | source)
XLA Modules:
  0.0 236.7 jit_solution(16197845670779278938)
XLA Ops:
  0.7 154.6 %exchange.1 = (f32[8,2,88,512]{3,2,1,0:T(8,128)}, f32[8,2,88,512]{3,2,1,0:T(8,128)}, f32[8,2,88,896]{3,2,1,0:T(8,128)}, f32[8,88,512]{2,1,0:T(8,128)}, f32[4,128...) custom-call(f32[8,704,512]{2,1,0:T(8,128)} %bitcast.16, bf16[8,704,512]{2,1,0:T(8,128)(2,1)} %bitcast.20, ...), custom_call_target="tpu_custom_call" | custom-call | tf_op jit(solution)/shard_map/exchange/pallas_call | solution.py:497
  155.3 61.9 %expert_update.1 = (f32[8,704,512]{2,1,0:T(8,128)}, f32[8,704,512]{2,1,0:T(8,128)}, f32[8,88,704]{2,1,0:T(8,128)}, f32[8,704,512]{2,1,0:T(8,128)}, f32[8,704,512...) custom-call(f32[8,704,512]{2,1,0:T(8,128)} %bitcast.24, ...), custom_call_target="tpu_custom_call" | custom-call | tf_op jit(solution)/shard_map/expert_update/pallas_call | solution.py:557
  217.2 19.3 %dense_update.1 = (f32[512,1024]{1,0:T(8,128)}, f32[512,1024]{1,0:T(8,128)}, f32[1024,128]{1,0:T(8,128)}, f32[512,1024]{1,0:T(8,128)}, f32[512,1024]{1,0:T(8,128...) custom-call(f32[512,1024]{1,0:T(8,128)} %refs_0_.1, ...), custom_call_target="tpu_custom_call" | custom-call | tf_op jit(solution)/shard_map/dense_update/pallas_call | solution.py:589

commit v4 on v3

--- a/solution.py
+++ b/solution.py
@@ -94,7 +94,7 @@
     dm, dg, dq = refs[9:21:3], refs[10:21:3], refs[11:21:3]
     o_pk, o_pf, o_sf, o_sd, o_pd, o_sfd, o_nrm = refs[21:28]
     (mk, gk, qk, md, gd, qd, mw, gw, qw,
-     pk, pk_in, pd, pd_c, pd_x, pf, sk, sk_c, sk_x, sf, sd, sd_in, wd, wd_in,
+     pk, pk_in, pd, pd_c, pd_x, pf, sk, sk_c, sk_x, sk_o, wk, wk_c, wk_x, sd, sd_in, wd, wd_in,
      pw, pw_in, sw, sw_c, sw_x, sfw, ae, li, aw, lw, nrm, nrm_y, nrm_d, nrm_f,
      ld, ldw, ldq, out_sem, outw_sem, remote, remote_w, remote_n) = refs[28:]
     t = lax.axis_index('tp')
@@ -111,10 +111,12 @@
 
     def expert_load(j, e, with_q):
         m_buf, g_buf, q_buf = (mk.at[j], gk.at[j], qk.at[j]) if j < 2 else (md, gd, qd)
-        copies = [pltpu.make_async_copy(em[j].at[e], m_buf, ld.at[j, 0]),
-                  pltpu.make_async_copy(eg[j].at[e], g_buf, ld.at[j, 1])]
+        slot = lax.rem(e, 2)
+        m_buf, g_buf, q_buf = m_buf.at[slot], g_buf.at[slot], q_buf.at[slot]
+        copies = [pltpu.make_async_copy(em[j].at[e], m_buf, ld.at[j, 0, slot]),
+                  pltpu.make_async_copy(eg[j].at[e], g_buf, ld.at[j, 1, slot])]
         if with_q:
-            copies.append(pltpu.make_async_copy(eq[j].at[e], q_buf, ld.at[j, 2]))
+            copies.append(pltpu.make_async_copy(eq[j].at[e], q_buf, ld.at[j, 2, slot]))
         return copies
 
     def start_all(copies):
@@ -174,10 +176,16 @@
         return send(sk.at[e, 1 - c], sk_c.at[e], 5, e, c_dev)
 
     def r_sk_x(e):
-        return send(sk.at[e, c], sk_x.at[e], 6, e, x_dev)
+        return send(sk.at[e, c], sk_x.at[e, :, 0:768], 6, e, x_dev)
 
     def r_sk_o(e):
-        return send(sf.at[e, c], sf.at[e, c], 7, e, c_dev)
+        return send(sk_x.at[e], sk_o.at[e], 7, e, c_dev)
+
+    def r_wk_c(e):
+        return send(wk.at[e, 1 - c], wk_c.at[e], 10, e, c_dev)
+
+    def r_wk_x(e):
+        return send(wk.at[e, c], wk_x.at[e], 11, e, x_dev)
 
     def r_sd(e):
         return send(sd.at[e], sd_in.at[e, :, 0:384], 8, e, y_dev)
@@ -203,8 +211,11 @@
     def out_pf(e):
         return pltpu.make_async_copy(pf.at[e], o_pf.at[e], out_sem.at[1, e])
 
-    def out_sf(e, j):
-        return pltpu.make_async_copy(sf.at[e, j], o_sf.at[e, j], out_sem.at[2 + j, e])
+    def out_own(e):
+        return pltpu.make_async_copy(sk_x.at[e], o_sf.at[e, c], out_sem.at[2, e])
+
+    def out_other(e):
+        return pltpu.make_async_copy(sk_o.at[e], o_sf.at[e, 1 - c], out_sem.at[3, e])
 
     def out_sd(e):
         return pltpu.make_async_copy(sd_in.at[e], o_sd.at[e], out_sem.at[4, e])
@@ -215,14 +226,16 @@
     def out_sfw(i):
         return pltpu.make_async_copy(sfw.at[i], o_sfd.at[i], outw_sem.at[1, i])
 
-    def block(j):
+    def block(j, e):
+        slot = lax.rem(e, 2)
         if j < 2:
-            return mk[j] + gk[j].astype(F32)
-        return md[...] + gd[...].astype(F32)
-
+            return mk[j, slot] + gk[j, slot].astype(F32)
+        return md[slot] + gd[slot].astype(F32)
+
+    for e in range(2):
+        for j in (2, 0, 1):
+            start_all(expert_load(j, e, True))
     dense_start(0, True)
-    for j in range(3):
-        start_all(expert_load(j, 0, True))
     pl.semaphore_wait(bar, 5)
 
     def dense_one(s, carry):
@@ -246,7 +259,6 @@
             r_pw(i).start()
         return carry
 
-    lax.fori_loop(0, 8, dense_one, 0)
 
     def pd_mid(e):
         r_pd_c(e).wait_recv()
@@ -256,12 +268,13 @@
     def expert_one(e, carry):
         for j in (2, 0, 1):
             wait_all(expert_load(j, e, True))
-            q = qk[j] if j < 2 else qd[...]
-            part = dot6(q, block(j), NN)
-
-            @pl.when(e < 7)
+            slot = lax.rem(e, 2)
+            q = qk[j, slot] if j < 2 else qd[slot]
+            part = dot6(q, block(j, e), NN)
+
+            @pl.when(e < 6)
             def _(j=j):
-                start_all(expert_load(j, e + 1, True))
+                start_all(expert_load(j, e + 2, True))
             if j < 2:
                 pk[e, j] = part
                 r_pk(e, j).start()
@@ -272,10 +285,13 @@
         pd_mid(e)
         return carry
 
-    lax.fori_loop(0, 8, expert_one, 0)
+    lax.fori_loop(0, 2, expert_one, 0)
+    lax.fori_loop(0, 8, dense_one, 0)
+    lax.fori_loop(2, 8, expert_one, 0)
+    for e in range(2):
+        for j in range(3):
+            start_all(expert_load(j, e, False))
     dense_start(0, False)
-    for j in range(3):
-        start_all(expert_load(j, 0, False))
 
     def dense_two(s, carry):
         slot = lax.rem(s, 2)
@@ -303,12 +319,6 @@
             r_sw_c(s // 4).start()
         return carry
 
-    lax.fori_loop(0, 8, dense_two, 0)
-    for d in range(2):
-        r_sw_c(d).wait_recv()
-        sw[2 * d + c] = sw[2 * d + c] + sw_c[d]
-        r_sw_x(d).start()
-
     def down_two(s, carry):
         @pl.when(s < 8)
         def _():
@@ -325,39 +335,58 @@
             total = jnp.concatenate([pf[e, 0], pf[e, 1]], axis=1)
             wd[e] = dot6(total, rows_to(total, 128), NT)
             r_wd(e).start()
-            sd[e] = dot6(total, rows_to(block(2), 384), NT)
-
-            @pl.when(e < 7)
+            sd[e] = dot6(total, rows_to(block(2, e), 384), NT)
+
+            @pl.when(e < 6)
             def _():
-                start_all(expert_load(2, e + 1, False))
-        return carry
-
-    lax.fori_loop(0, 9, down_two, 0)
+                start_all(expert_load(2, e + 2, False))
+        return carry
 
     def sd_send(e, carry):
         r_sd(e).start()
         return carry
 
-    lax.fori_loop(0, 8, sd_send, 0)
+    def sk_mid(e):
+        r_sk_c(e).wait_recv()
+        sk[e, c] = sk[e, c] + sk_c[e]
+        r_sk_x(e).start()
 
     def keep_two(e, carry):
         for j in range(2):
             r_pk(e, j).wait_recv()
             total = pk[e, j] + pk_in[e, j]
             pk_in[e, j] = total
+            wk[e, j] = dot6(total, rows_to(total, 128), NT)
+        r_wk_c(e).start()
+        out_pk(e).start()
+        for j in range(2):
             wait_all(expert_load(j, e, False))
-            sk[e, j, :, 768:] = dot6(total, rows_to(total, 128), NT)
-            sk[e, j, :, :768] = dot6(total, rows_to(block(j), 768), NT)
-
-            @pl.when(e < 7)
+            sk[e, j] = dot6(pk_in[e, j], rows_to(block(j, e), 768), NT)
+
+            @pl.when(e < 6)
             def _(j=j):
-                start_all(expert_load(j, e + 1, False))
+                start_all(expert_load(j, e + 2, False))
         r_sk_c(e).start()
-        out_pk(e).start()
-        r_sk_c(e).wait_recv()
-        sk[e, c] = sk[e, c] + sk_c[e]
-        r_sk_x(e).start()
-        return carry
+        r_wk_c(e).wait_recv()
+        wk[e, c] = wk[e, c] + wk_c[e]
+        r_wk_x(e).start()
+
+        @pl.when(e > 3)
+        def _():
+            sk_mid(e - 2)
+        return carry
+
+    lax.fori_loop(0, 2, keep_two, 0)
+    sk_mid(0)
+    sk_mid(1)
+    lax.fori_loop(0, 9, down_two, 0)
+    lax.fori_loop(0, 8, sd_send, 0)
+    lax.fori_loop(0, 8, dense_two, 0)
+    for d in range(2):
+        r_sw_c(d).wait_recv()
+        sw[2 * d + c] = sw[2 * d + c] + sw_c[d]
+        r_sw_x(d).start()
+
 
     nrm[...] = jnp.zeros((128, LANES), F32)
     lane_full = lax.broadcasted_iota(jnp.int32, (128, LANES), 1)
@@ -366,7 +395,7 @@
         sq = rows_to(jnp.sum(rt * rt, axis=1, keepdims=True), 128)
         nrm[...] = jnp.where(lane_full == where, sq, nrm[...])
 
-    lax.fori_loop(0, 4, keep_two, 0)
+    lax.fori_loop(2, 6, keep_two, 0)
 
     for d in range(2):
         r_sw_x(d).wait_recv()
@@ -383,7 +412,9 @@
         add_norm(rt, 24 + i)
         r_sw_o(d).start()
 
-    lax.fori_loop(4, 8, keep_two, 0)
+    lax.fori_loop(6, 8, keep_two, 0)
+    sk_mid(6)
+    sk_mid(7)
 
     for e in range(8):
         r_wd(e).wait_recv()
@@ -392,24 +423,21 @@
     for e in range(8):
         sd_in[e, :, 384:] = li[:, e, :]
 
-    def keep_total(e, carry):
-        r_sk_x(e).wait_recv()
-        sf[e, c] = sk[e, c] + sk_x[e]
-        return carry
-
-    lax.fori_loop(0, 8, keep_total, 0)
     for e in range(8):
-        ae[:, e, :] = sf[e, c, :, 768:]
+        r_wk_x(e).wait_recv()
+        ae[:, e, :] = wk[e, c] + wk_x[e]
     eliminate(ae, li, 88)
     for e in range(8):
-        sf[e, c, :, 768:] = li[:, e, :]
+        sk_x[e, :, 768:] = li[:, e, :]
 
     def keep_r(e, carry):
-        rt = dot6(sf[e, c, :, 768:], rows_to(sf[e, c, :, :768], 128), NN)
-        sf[e, c, :, :768] = rt
+        r_sk_x(e).wait_recv()
+        st = sk[e, c] + sk_x[e, :, :768]
+        rt = dot6(sk_x[e, :, 768:], rows_to(st, 128), NN)
+        sk_x[e, :, :768] = rt
+        r_sk_o(e).start()
         add_norm(rt, 8 * c + e)
-        r_sk_o(e).start()
-        out_sf(e, c).start()
+        out_own(e).start()
         return carry
 
     lax.fori_loop(0, 8, keep_r, 0)
@@ -432,7 +460,7 @@
 
     def finish(e, carry):
         r_sk_o(e).wait_recv()
-        out_sf(e, 1 - c).start()
+        out_other(e).start()
         return carry
 
     lax.fori_loop(0, 8, finish, 0)
@@ -456,9 +484,9 @@
     last.start()
 
     def drain(e, carry):
-        for r in (r_pk(e, 0), r_pk(e, 1), r_pd_c(e), r_pd_x(e), r_pd_o(e), r_sk_c(e), r_sk_x(e), r_sk_o(e), r_sd(e), r_wd(e)):
+        for r in (r_pk(e, 0), r_pk(e, 1), r_pd_c(e), r_pd_x(e), r_pd_o(e), r_sk_c(e), r_sk_x(e), r_sk_o(e), r_sd(e), r_wd(e), r_wk_c(e), r_wk_x(e)):
             r.wait_send()
-        for o in (out_pk(e), out_pf(e), out_sf(e, 0), out_sf(e, 1), out_sd(e)):
+        for o in (out_pk(e), out_pf(e), out_own(e), out_other(e), out_sd(e)):
             o.wait()
         return carry
 
@@ -483,17 +511,18 @@
     def v(*shape, dtype=F32):
         return pltpu.VMEM(shape, dtype)
 
-    scratch = [v(2, 704, 512), v(2, 704, 512, dtype=BF), v(2, 88, 704),
-               v(352, 1024), v(352, 1024, dtype=BF), v(88, 352),
+    scratch = [v(2, 2, 704, 512), v(2, 2, 704, 512, dtype=BF), v(2, 2, 88, 704),
+               v(2, 352, 1024), v(2, 352, 1024, dtype=BF), v(2, 88, 352),
                v(2, 256, 1024), v(2, 256, 1024, dtype=BF), v(2, 1024, 128),
                v(8, 2, 88, 512), v(8, 2, 88, 512),
                v(8, 2, 88, 512), v(8, 88, 512), v(8, 88, 512), v(8, 2, 88, 512),
-               v(8, 2, 88, 896), v(8, 88, 896), v(8, 88, 896), v(8, 2, 88, 896),
+               v(8, 2, 88, 768), v(8, 88, 768), v(8, 88, 896), v(8, 88, 896),
+               v(8, 2, 88, 128), v(8, 88, 128), v(8, 88, 128),
                v(8, 88, 384), v(8, 88, 512), v(8, 88, 128), v(8, 88, 128),
                v(4, 128, 512), v(4, 128, 512), v(4, 128, 1152), v(2, 128, 1152), v(2, 128, 1152), v(4, 128, 1152),
                v(88, 8, 128), v(88, 8, 128), v(128, 8, 128), v(128, 8, 128),
                v(128, 128), v(128, 128), v(128, 128), v(3, 128, 128),
-               dma((3, 3)), dma((2, 2)), dma((2,)), dma((5, 8)), dma((2, 5)), dma((2, 10, 8)), dma((2, 4, 4)), dma((2, 5))]
+               dma((3, 3, 2)), dma((2, 2)), dma((2,)), dma((5, 8)), dma((2, 5)), dma((2, 12, 8)), dma((2, 4, 4)), dma((2, 5))]
     return pl.pallas_call(
         exchange_kernel,
         in_specs=[any_spec] * len(args), out_specs=[any_spec] * len(shapes),

time: 237 us -> 237 us (level)
  no operation moved by 1% of the time
where the time goes in v4:
time: 237 us; the launch traced here: 236 us
  Pallas kernels  235 us (99%)
    pallas_call x1, Pallas kernels, exchange(): pl.pallas_call(exchange_kernel, in_specs=[any_spec] * len(args), out_spec...  154 us
    pallas_call x1, Pallas kernels, expert_update(): pl.pallas_call(expert_kernel, grid=(8,), in_specs=in_specs, out_specs=[bl...  62 us
    pallas_call x1, Pallas kernels, dense_update(): pl.pallas_call(dense_kernel, grid=(DENSE_STEPS,), in_specs=in_specs, out_...  19.1 us

profile of v4, /device:TPU:0, one launch (start us, length us, event | category | flops | bytes accessed | tf_op | source)
XLA Modules:
  0.0 236.2 jit_solution(4407715266615197538)
XLA Ops:
  0.7 154.3 %exchange.1 = (f32[8,2,88,512]{3,2,1,0:T(8,128)}, f32[8,2,88,512]{3,2,1,0:T(8,128)}, f32[8,2,88,896]{3,2,1,0:T(8,128)}, f32[8,88,512]{2,1,0:T(8,128)}, f32[4,128...) custom-call(f32[8,704,512]{2,1,0:T(8,128)} %bitcast.16, bf16[8,704,512]{2,1,0:T(8,128)(2,1)} %bitcast.20, ...), custom_call_target="tpu_custom_call" | custom-call | tf_op jit(solution)/shard_map/exchange/pallas_call | solution.py:526
  155.0 62.0 %expert_update.1 = (f32[8,704,512]{2,1,0:T(8,128)}, f32[8,704,512]{2,1,0:T(8,128)}, f32[8,88,704]{2,1,0:T(8,128)}, f32[8,704,512]{2,1,0:T(8,128)}, f32[8,704,512...) custom-call(f32[8,704,512]{2,1,0:T(8,128)} %bitcast.24, ...), custom_call_target="tpu_custom_call" | custom-call | tf_op jit(solution)/shard_map/expert_update/pallas_call | solution.py:586
  217.0 19.1 %dense_update.1 = (f32[512,1024]{1,0:T(8,128)}, f32[512,1024]{1,0:T(8,128)}, f32[1024,128]{1,0:T(8,128)}, f32[512,1024]{1,0:T(8,128)}, f32[512,1024]{1,0:T(8,128...) custom-call(f32[512,1024]{1,0:T(8,128)} %refs_0_.1, ...), custom_call_target="tpu_custom_call" | custom-call | tf_op jit(solution)/shard_map/dense_update/pallas_call | solution.py:618

commit v5 on v4

--- a/solution.py
+++ b/solution.py
@@ -87,6 +87,9 @@
                 below(k0 + 8, rank - k0 - 8, False)
             return carry
         lax.fori_loop(0, 4, step, 0)
+
+
+HELD = 5
 
 
 def exchange_kernel(*refs):
@@ -277,7 +280,10 @@
                 start_all(expert_load(j, e + 2, True))
             if j < 2:
                 pk[e, j] = part
-                r_pk(e, j).start()
+
+                @pl.when(e < HELD)
+                def _(j=j):
+                    r_pk(e, j).start()
             else:
                 pd[e, 0] = part[:, :512]
                 pd[e, 1] = part[:, 512:]
@@ -380,6 +386,9 @@
     sk_mid(0)
     sk_mid(1)
     lax.fori_loop(0, 9, down_two, 0)
+    for e in range(HELD, 8):
+        r_pk(e, 0).start()
+        r_pk(e, 1).start()
     lax.fori_loop(0, 8, sd_send, 0)
     lax.fori_loop(0, 8, dense_two, 0)
     for d in range(2):
@@ -395,7 +404,16 @@
         sq = rows_to(jnp.sum(rt * rt, axis=1, keepdims=True), 128)
         nrm[...] = jnp.where(lane_full == where, sq, nrm[...])
 
-    lax.fori_loop(2, 6, keep_two, 0)
+    lax.fori_loop(2, 5, keep_two, 0)
+
+    for e in range(8):
+        r_wd(e).wait_recv()
+        ae[:, e, :] = wd[e] + wd_in[e]
+    eliminate(ae, li, 88)
+    for e in range(8):
+        sd_in[e, :, 384:] = li[:, e, :]
+
+    lax.fori_loop(5, 6, keep_two, 0)
 
     for d in range(2):
         r_sw_x(d).wait_recv()
@@ -415,13 +433,6 @@
     lax.fori_loop(6, 8, keep_two, 0)
     sk_mid(6)
     sk_mid(7)
-
-    for e in range(8):
-        r_wd(e).wait_recv()
-        ae[:, e, :] = wd[e] + wd_in[e]
-    eliminate(ae, li, 88)
-    for e in range(8):
-        sd_in[e, :, 384:] = li[:, e, :]
 
     for e in range(8):
         r_wk_x(e).wait_recv()
@@ -594,30 +605,40 @@
 
 
 def dense_kernel(*refs):
-    pw, sfw, dinv_ref = refs[12:15]
-    part = pl.program_id(0)
+    pw, linv, rt_ref, dinv_ref = refs[12:16]
+    left = refs[28]
+
+    @pl.when(pl.program_id(0) == 0)
+    def _():
+        for i in range(4):
+            left[i] = left_cat(dot6(linv[i], pw[i], NN))
+
     for i in range(4):
         x_ref, m_ref, g_ref = refs[3 * i:3 * i + 3]
-        x_out, m_out, q_out = refs[15 + 3 * i:18 + 3 * i]
-        dinv = take_col(dinv_ref, 128, 24 + i)
-        pt = dot6(sfw[i, :, 1024:], pw[i], NN)
-        apply_update(x_ref, m_ref, g_ref, pt, sfw[i, :, :1024], dinv, x_out, m_out, LEARN_RATE)
-        q_rows = q_out.shape[0]
-        q_out[...] = (sfw[i, :, pl.ds(pl.multiple_of(part * q_rows, q_rows), q_rows)] * dinv).T
+        x_out, m_out, q_out = refs[16 + 3 * i:19 + 3 * i]
+        rt = rt_ref[i]
+        qt = rt * take_col(dinv_ref, 128, 24 + i)
+        b = m_ref[...] + g_ref[...].astype(F32)
+        m_out[...] = b - (1.0 - MOMENTUM) * jnp.dot(left[i], right_cat(rt), preferred_element_type=F32)
+        x_out[...] = x_ref[...] - LEARN_RATE * jnp.dot(left[i], right_cat(qt), preferred_element_type=F32)
+        q_out[...] = qt.T
 
 
 def dense_update(mats, pw, sfw, dinv):
-    args = [a for grp in mats for a in grp] + [pw, sfw, dinv]
+    args = [a for grp in mats for a in grp] + [pw, sfw, sfw, dinv]
     rows, cols = mats[0][0].shape
-    blk = pl.BlockSpec((rows // DENSE_STEPS, cols), lambda s: (s, 0))
-    q_blk = pl.BlockSpec((cols // DENSE_STEPS, 128), lambda s: (s, 0))
-    in_specs = [blk] * 12 + [pl.BlockSpec((4, 128, rows // DENSE_STEPS), lambda s: (0, 0, s)),
-                             pl.BlockSpec(sfw.shape, lambda s: (0, 0, 0)),
+    wide = cols // DENSE_STEPS
+    blk = pl.BlockSpec((rows, wide), lambda s: (0, s))
+    q_blk = pl.BlockSpec((wide, 128), lambda s: (s, 0))
+    in_specs = [blk] * 12 + [pl.BlockSpec(pw.shape, lambda s: (0, 0, 0)),
+                             pl.BlockSpec((4, 128, 128), lambda s: (0, 0, 8)),
+                             pl.BlockSpec((4, 128, wide), lambda s: (0, 0, s)),
                              pl.BlockSpec(dinv.shape, lambda s: (0, 0))]
     w_out = jax.ShapeDtypeStruct((rows, cols), F32)
     return pl.pallas_call(
         dense_kernel, grid=(DENSE_STEPS,), in_specs=in_specs, out_specs=[blk, blk, q_blk] * 4,
         out_shape=[w_out, w_out, jax.ShapeDtypeStruct((cols, 128), F32)] * 4,
+        scratch_shapes=[pltpu.VMEM((4, rows, 6 * LANES), BF)],
         compiler_params=pltpu.CompilerParams(vmem_limit_bytes=60 * MIB),
         name='dense_update',
     )(*args)

time: 237 us -> 233 us (0.983)
  Pallas kernels: 235 us -> 232 us
where the time goes in v5:
time: 233 us
  Pallas kernels  232 us (100%)
    pallas_call x1, Pallas kernels, exchange(): pl.pallas_call(exchange_kernel, in_specs=[any_spec] * len(args), out_spec...  153 us
    pallas_call x1, Pallas kernels, expert_update(): pl.pallas_call(expert_kernel, grid=(8,), in_specs=in_specs, out_specs=[bl...  61.8 us
    pallas_call x1, Pallas kernels, dense_update(): pl.pallas_call(dense_kernel, grid=(DENSE_STEPS,), in_specs=in_specs, out_...  17.8 us

profile of v5, /device:TPU:0, one launch (start us, length us, event | category | flops | bytes accessed | tf_op | source)
XLA Modules:
  0.0 233.1 jit_solution(14045376922274560928)
XLA Ops:
  0.7 152.7 %exchange.1 = (f32[8,2,88,512]{3,2,1,0:T(8,128)}, f32[8,2,88,512]{3,2,1,0:T(8,128)}, f32[8,2,88,896]{3,2,1,0:T(8,128)}, f32[8,88,512]{2,1,0:T(8,128)}, f32[4,128...) custom-call(f32[8,704,512]{2,1,0:T(8,128)} %bitcast.16, bf16[8,704,512]{2,1,0:T(8,128)(2,1)} %bitcast.20, ...), custom_call_target="tpu_custom_call" | custom-call | tf_op jit(solution)/shard_map/exchange/pallas_call | solution.py:537
  153.3 61.8 %expert_update.1 = (f32[8,704,512]{2,1,0:T(8,128)}, f32[8,704,512]{2,1,0:T(8,128)}, f32[8,88,704]{2,1,0:T(8,128)}, f32[8,704,512]{2,1,0:T(8,128)}, f32[8,704,512...) custom-call(f32[8,704,512]{2,1,0:T(8,128)} %bitcast.24, ...), custom_call_target="tpu_custom_call" | custom-call | tf_op jit(solution)/shard_map/expert_update/pallas_call | solution.py:597
  215.1 17.8 %dense_update.1 = (f32[512,1024]{1,0:T(8,128)}, f32[512,1024]{1,0:T(8,128)}, f32[1024,128]{1,0:T(8,128)}, f32[512,1024]{1,0:T(8,128)}, f32[512,1024]{1,0:T(8,128...) custom-call(f32[512,1024]{1,0:T(8,128)} %refs_0_.1, ...), custom_call_target="tpu_custom_call" | custom-call | tf_op jit(solution)/shard_map/dense_update/pallas_call | solution.py:638

commit v6 on v5

--- a/solution.py
+++ b/solution.py
@@ -32,11 +32,11 @@
     return jnp.concatenate([x, jnp.zeros((rows - have, cols), x.dtype)], axis=0)
 
 
-def dot6(left, right, dims):
+def dot6(left, right, dims, grow=0):
     rank = left.shape[0]
     pad = -(-rank // 16) * 16
     lh, lm, ll = split3(rows_to(left, pad))
-    rh, rm, rl = split3(right)
+    rh, rm, rl = (rows_to(term, grow) if grow else term for term in split3(right))
     with_h = lax.dot_general(jnp.concatenate([lh, lm, ll], axis=0), rh, dims, preferred_element_type=F32)
     with_m = lax.dot_general(jnp.concatenate([lh, lm], axis=0), rm, dims, preferred_element_type=F32)
     with_l = lax.dot_general(lh, rl, dims, preferred_element_type=F32)
@@ -341,7 +341,7 @@
             total = jnp.concatenate([pf[e, 0], pf[e, 1]], axis=1)
             wd[e] = dot6(total, rows_to(total, 128), NT)
             r_wd(e).start()
-            sd[e] = dot6(total, rows_to(block(2, e), 384), NT)
+            sd[e] = dot6(total, block(2, e), NT, 384)
 
             @pl.when(e < 6)
             def _():
@@ -367,7 +367,7 @@
         out_pk(e).start()
         for j in range(2):
             wait_all(expert_load(j, e, False))
-            sk[e, j] = dot6(pk_in[e, j], rows_to(block(j, e), 768), NT)
+            sk[e, j] = dot6(pk_in[e, j], block(j, e), NT, 768)
 
             @pl.when(e < 6)
             def _(j=j):

time: 233 us -> 233 us (level)
  no operation moved by 1% of the time
where the time goes in v6:
time: 233 us
  Pallas kernels  232 us (100%)
    pallas_call x1, Pallas kernels, exchange(): pl.pallas_call(exchange_kernel, in_specs=[any_spec] * len(args), out_spec...  152 us
    pallas_call x1, Pallas kernels, expert_update(): pl.pallas_call(expert_kernel, grid=(8,), in_specs=in_specs, out_specs=[bl...  61.8 us
    pallas_call x1, Pallas kernels, dense_update(): pl.pallas_call(dense_kernel, grid=(DENSE_STEPS,), in_specs=in_specs, out_...  17.8 us

profile of v6, /device:TPU:0, one launch (start us, length us, event | category | flops | bytes accessed | tf_op | source)
XLA Modules:
  0.0 232.6 jit_solution(472558502107042141)
XLA Ops:
  0.7 152.1 %exchange.1 = (f32[8,2,88,512]{3,2,1,0:T(8,128)}, f32[8,2,88,512]{3,2,1,0:T(8,128)}, f32[8,2,88,896]{3,2,1,0:T(8,128)}, f32[8,88,512]{2,1,0:T(8,128)}, f32[4,128...) custom-call(f32[8,704,512]{2,1,0:T(8,128)} %bitcast.16, bf16[8,704,512]{2,1,0:T(8,128)(2,1)} %bitcast.20, ...), custom_call_target="tpu_custom_call" | custom-call | tf_op jit(solution)/shard_map/exchange/pallas_call | solution.py:537
  152.8 61.8 %expert_update.1 = (f32[8,704,512]{2,1,0:T(8,128)}, f32[8,704,512]{2,1,0:T(8,128)}, f32[8,88,704]{2,1,0:T(8,128)}, f32[8,704,512]{2,1,0:T(8,128)}, f32[8,704,512...) custom-call(f32[8,704,512]{2,1,0:T(8,128)} %bitcast.24, ...), custom_call_target="tpu_custom_call" | custom-call | tf_op jit(solution)/shard_map/expert_update/pallas_call | solution.py:597
  214.6 17.8 %dense_update.1 = (f32[512,1024]{1,0:T(8,128)}, f32[512,1024]{1,0:T(8,128)}, f32[1024,128]{1,0:T(8,128)}, f32[512,1024]{1,0:T(8,128)}, f32[512,1024]{1,0:T(8,128...) custom-call(f32[512,1024]{1,0:T(8,128)} %refs_0_.1, ...), custom_call_target="tpu_custom_call" | custom-call | tf_op jit(solution)/shard_map/dense_update/pallas_call | solution.py:638
